TPU v7x, 32 devices: a whole 2x2x4 slice. The times are simulated.
32 devices in a mesh: fsdp: 4 (over x, core), ctx: 8 (over z, y).
Axes of the slice: x: 2, y: 2, z: 4, core: 2. Of those that a mesh axis runs over, the one named last changes fastest.
Arguments:
- inputs: bfloat16 [8, 1024, 1600], P('fsdp', 'ctx'), may hold values from -6 to 6
- cotangent: bfloat16 [8, 1024, 1600], P('fsdp', 'ctx'), may hold values from -6 to 6
- segments: int32 [8, 1024], P('fsdp', 'ctx'), may hold values from 0 to 10, as said below
- stretch_order: int32 [8], replicated, may hold values from 0 to 7, as said below
- prenorm_gain: bfloat16 [1600], P('ctx'), may hold values from 0.5 to 1.5
- prenorm_shift: bfloat16 [1600], P('ctx'), may hold values from -2 to 2
- joint_weight: bfloat16 [1600, 4800], P('fsdp', 'ctx')
- query_bias: bfloat16 [1600], P('ctx'), may hold values from -2 to 2
- value_bias: bfloat16 [1600], P('ctx'), may hold values from -2 to 2
- mixer_weight: bfloat16 [1600, 1600], P('fsdp', 'ctx'), may hold values from -0.75 to 0.75
- mixer_bias: bfloat16 [1600], P('ctx'), may hold values from -2 to 2
- midnorm_gain: bfloat16 [1600], P('ctx'), may hold values from 0.5 to 1.5
- midnorm_shift: bfloat16 [1600], P('ctx'), may hold values from -2 to 2
- expand_weight: bfloat16 [1600, 6400], P('fsdp', 'ctx'), may hold values from -0.15625 to 0.15625
- expand_bias: bfloat16 [6400], P('ctx'), may hold values from -2 to 2
- shrink_weight: bfloat16 [6400, 1600], P('fsdp', 'ctx'), may hold values from -0.078125 to 0.078125
- shrink_bias: bfloat16 [1600], P('ctx'), may hold values from -2 to 2
Outputs:
- block_output: bfloat16 [8, 1024, 1600], P('fsdp', 'ctx')
- input_gradient: float32 [8, 1024, 1600], P('fsdp', 'ctx')
- prenormgain_gradient: float32 [1600], P('ctx')
- prenormshift_gradient: float32 [1600], P('ctx')
- joint_gradient: float32 [1600, 4800], P('fsdp', 'ctx')
- querybias_gradient: float32 [1600], P('ctx')
- valuebias_gradient: float32 [1600], P('ctx')
- mixer_gradient: float32 [1600, 1600], P('fsdp', 'ctx')
- mixerbias_gradient: float32 [1600], P('ctx')
- midnormgain_gradient: float32 [1600], P('ctx')
- midnormshift_gradient: float32 [1600], P('ctx')
- expand_gradient: float32 [1600, 6400], P('fsdp', 'ctx')
- expandbias_gradient: float32 [6400], P('ctx')
- shrink_gradient: float32 [6400, 1600], P('fsdp', 'ctx')
- shrinkbias_gradient: float32 [1600], P('ctx')
Inputs may be any that keep to these rules, and one draw needn't show every extreme that they name: A permutation: stored block i of every sequence is its true block stretch_order[i]. `segments`: in true order the numbers start at 0 and rise by one where a document starts; each document but a sequence's last spans 100 to 1000 positions.
All inputs are finite; a program needn't handle non-finite values.
Results may differ from a plain program's by a relative error of at most 0.019.
Values may be sent and summed in bfloat16 or wider, within the bound.
A program may use at most 320 MiB of HBM per device.

v0:
```python
import jax
import jax.numpy as jnp
from jax import lax
from jax.sharding import PartitionSpec as P

HEAD = 64
MICRO = 2


epsilon = 1e-05
masked_score = -1e30


def layer_norm(values, gain, shift):
    center = values - jnp.mean(values, axis=-1, keepdims=True)
    spread = jnp.mean(center * center, axis=-1, keepdims=True)
    return center * lax.rsqrt(spread + epsilon) * gain + shift


def piece_size(count):
    size_now = min(count, 512)
    while count % size_now:
        size_now -= 1
    return size_now


def true_positions(stretch_order, first_index, count, stretch_len):
    stored = first_index + jnp.arange(count, dtype=jnp.int32)
    holder = stored // stretch_len
    picked = holder[:, None] == jnp.arange(stretch_order.shape[0], dtype=jnp.int32)[None, :]
    return (
        jnp.sum(jnp.where(picked, stretch_order[None, :], 0), axis=1) * stretch_len
        + stored % stretch_len
    )


def times_transposed(left, right):
    return lax.dot_general(
        left, right, (((1,), (1,)), ((), ())), preferred_element_type=jnp.float32
    )


def outer_sum(left, right):
    return lax.dot_general(
        left, right, (((0,), (0,)), ((), ())), preferred_element_type=jnp.float32
    )


def fetch_weights(local_parts):
    (
        joint_weight,
        mixer_weight,
        expand_weight,
        shrink_weight,
        prenorm_gain,
        prenorm_shift,
        query_bias,
        value_bias,
        mixer_bias,
        midnorm_gain,
        midnorm_shift,
        expand_bias,
        shrink_bias,
    ) = local_parts
    spread_out = (
        lax.all_gather(joint_weight, "ctx", axis=1, tiled=True),
        lax.all_gather(mixer_weight, "ctx", axis=1, tiled=True),
        lax.all_gather(expand_weight, "ctx", axis=1, tiled=True),
        lax.all_gather(shrink_weight, "ctx", axis=1, tiled=True),
        lax.all_gather(prenorm_gain, "ctx", axis=0, tiled=True),
        lax.all_gather(prenorm_shift, "ctx", axis=0, tiled=True),
        lax.all_gather(query_bias, "ctx", axis=0, tiled=True),
        lax.all_gather(value_bias, "ctx", axis=0, tiled=True),
        lax.all_gather(mixer_bias, "ctx", axis=0, tiled=True),
        lax.all_gather(midnorm_gain, "ctx", axis=0, tiled=True),
        lax.all_gather(midnorm_shift, "ctx", axis=0, tiled=True),
        lax.all_gather(expand_bias, "ctx", axis=0, tiled=True),
        lax.all_gather(shrink_bias, "ctx", axis=0, tiled=True),
    )
    whole_rows = (
        lax.all_gather(spread_out[0], "fsdp", axis=0, tiled=True),
        lax.all_gather(spread_out[1], "fsdp", axis=0, tiled=True),
        lax.all_gather(spread_out[2], "fsdp", axis=0, tiled=True),
        lax.all_gather(spread_out[3], "fsdp", axis=0, tiled=True),
    )
    return tuple(whole_rows) + tuple(spread_out[4:])


def reduce_gradients(matrices, smalls):
    small_sums = (
        lax.psum(smalls[0].astype(jnp.bfloat16), "fsdp").astype(jnp.float32),
        lax.psum(smalls[1].astype(jnp.bfloat16), "fsdp").astype(jnp.float32),
        lax.psum(smalls[2].astype(jnp.bfloat16), "fsdp").astype(jnp.float32),
        lax.psum(smalls[3].astype(jnp.bfloat16), "fsdp").astype(jnp.float32),
        lax.psum(smalls[4].astype(jnp.bfloat16), "fsdp").astype(jnp.float32),
        lax.psum(smalls[5].astype(jnp.bfloat16), "fsdp").astype(jnp.float32),
        lax.psum(smalls[6].astype(jnp.bfloat16), "fsdp").astype(jnp.float32),
        lax.psum(smalls[7].astype(jnp.bfloat16), "fsdp").astype(jnp.float32),
        lax.psum(smalls[8].astype(jnp.bfloat16), "fsdp").astype(jnp.float32),
    )
    column_part = (
        lax.psum_scatter(
            matrices[0].astype(jnp.bfloat16), "ctx", scatter_dimension=1, tiled=True
        ).astype(jnp.float32),
        lax.psum_scatter(
            matrices[1].astype(jnp.bfloat16), "ctx", scatter_dimension=1, tiled=True
        ).astype(jnp.float32),
        lax.psum_scatter(
            matrices[2].astype(jnp.bfloat16), "ctx", scatter_dimension=1, tiled=True
        ).astype(jnp.float32),
        lax.psum_scatter(
            matrices[3].astype(jnp.bfloat16), "ctx", scatter_dimension=1, tiled=True
        ).astype(jnp.float32),
        lax.psum_scatter(
            small_sums[0].astype(jnp.bfloat16), "ctx", scatter_dimension=0, tiled=True
        ).astype(jnp.float32),
        lax.psum_scatter(
            small_sums[1].astype(jnp.bfloat16), "ctx", scatter_dimension=0, tiled=True
        ).astype(jnp.float32),
        lax.psum_scatter(
            small_sums[2].astype(jnp.bfloat16), "ctx", scatter_dimension=0, tiled=True
        ).astype(jnp.float32),
        lax.psum_scatter(
            small_sums[3].astype(jnp.bfloat16), "ctx", scatter_dimension=0, tiled=True
        ).astype(jnp.float32),
        lax.psum_scatter(
            small_sums[4].astype(jnp.bfloat16), "ctx", scatter_dimension=0, tiled=True
        ).astype(jnp.float32),
        lax.psum_scatter(
            small_sums[5].astype(jnp.bfloat16), "ctx", scatter_dimension=0, tiled=True
        ).astype(jnp.float32),
        lax.psum_scatter(
            small_sums[6].astype(jnp.bfloat16), "ctx", scatter_dimension=0, tiled=True
        ).astype(jnp.float32),
        lax.psum_scatter(
            small_sums[7].astype(jnp.bfloat16), "ctx", scatter_dimension=0, tiled=True
        ).astype(jnp.float32),
        lax.psum_scatter(
            small_sums[8].astype(jnp.bfloat16), "ctx", scatter_dimension=0, tiled=True
        ).astype(jnp.float32),
    )
    row_part = (
        lax.psum_scatter(
            column_part[0].astype(jnp.bfloat16), "fsdp", scatter_dimension=0, tiled=True
        ).astype(jnp.float32),
        lax.psum_scatter(
            column_part[1].astype(jnp.bfloat16), "fsdp", scatter_dimension=0, tiled=True
        ).astype(jnp.float32),
        lax.psum_scatter(
            column_part[2].astype(jnp.bfloat16), "fsdp", scatter_dimension=0, tiled=True
        ).astype(jnp.float32),
        lax.psum_scatter(
            column_part[3].astype(jnp.bfloat16), "fsdp", scatter_dimension=0, tiled=True
        ).astype(jnp.float32),
    )
    return tuple(row_part) + tuple(column_part[4:])


def local(
    inputs,
    cotangent,
    segments,
    stretch_order,
    prenorm_gain,
    prenorm_shift,
    joint_weight,
    query_bias,
    value_bias,
    mixer_weight,
    mixer_bias,
    midnorm_gain,
    midnorm_shift,
    expand_weight,
    expand_bias,
    shrink_weight,
    shrink_bias,
):
    local_parts = (
        joint_weight,
        mixer_weight,
        expand_weight,
        shrink_weight,
        prenorm_gain,
        prenorm_shift,
        query_bias,
        value_bias,
        mixer_bias,
        midnorm_gain,
        midnorm_shift,
        expand_bias,
        shrink_bias,
    )
    seq_local, stretch_len, model_width = inputs.shape
    head_count = model_width // HEAD
    group_size = seq_local // MICRO
    row_count = group_size * stretch_len
    score_scale = HEAD ** (-0.5)
    ctx_place = lax.axis_index("ctx")
    own_stretch = jnp.sum(
        jnp.where(
            jnp.arange(stretch_order.shape[0], dtype=jnp.int32) == ctx_place, stretch_order, 0
        )
    )
    own_pos = own_stretch * stretch_len + jnp.arange(stretch_len, dtype=jnp.int32)
    all_segments = lax.all_gather(segments, "ctx", axis=1, tiled=True)

    def backward_micro(weights, kept_values, micro_index):
        (
            joint_full,
            mixer_full,
            expand_full,
            shrink_full,
            gain_one,
            shift_one,
            qbias_full,
            vbias_full,
            mbias_full,
            gain_two,
            shift_two,
            ebias_full,
            sbias_full,
        ) = weights
        (
            tokens,
            seg_local,
            seg_whole,
            normed,
            queries,
            keys_local,
            values_local,
            mixed_rows,
            attended,
            log_total,
            middle,
            second,
            expanded,
            active,
        ) = kept_values
        lower = micro_index * group_size
        tangent_rows = cotangent[lower : lower + group_size].reshape(row_count, model_width)
        active_grad = times_transposed(tangent_rows, shrink_full)
        gelu_pull = jax.vjp(lambda value_in: jax.nn.gelu(value_in, approximate=True), expanded)[1]
        expand_delta = gelu_pull(active_grad)[0].astype(jnp.bfloat16)
        second_grad = times_transposed(expand_delta, expand_full)
        mid_pull = jax.vjp(
            layer_norm, middle, gain_two.astype(jnp.float32), shift_two.astype(jnp.float32)
        )[1]
        middle_grad, gain_two_grad, shift_two_grad = mid_pull(second_grad)
        middle_grad = middle_grad + tangent_rows.astype(jnp.float32)
        branch_delta = middle_grad.astype(jnp.bfloat16)
        attended_delta = times_transposed(branch_delta, mixer_full).astype(jnp.bfloat16)
        grad_heads = attended_delta.reshape(group_size, stretch_len, head_count, HEAD)
        delta_heads = jnp.sum(
            grad_heads.transpose(0, 2, 1, 3).astype(jnp.float32) * attended, axis=-1
        )
        delta_rows = delta_heads.transpose(0, 2, 1)
        log_rows = log_total.transpose(0, 2, 1)
        lse_whole, delta_whole = (
            lax.all_gather(log_rows, "ctx", axis=1, tiled=True),
            lax.all_gather(delta_rows, "ctx", axis=1, tiled=True),
        )
        query_heads = queries.reshape(group_size, stretch_len, head_count, HEAD)
        key_heads = keys_local.reshape(group_size, stretch_len, head_count, HEAD)
        value_heads = values_local.reshape(group_size, stretch_len, head_count, HEAD)
        head_zeros = jnp.zeros((group_size, head_count, stretch_len, HEAD), jnp.float32)
        query_key_piece = lax.all_gather(keys_local, "ctx", axis=1, tiled=True)
        value_piece = lax.all_gather(values_local, "ctx", axis=1, tiled=True)
        count = query_key_piece.shape[1]
        step_len = piece_size(count)

        def query_block_step(turn_index, running):
            offset = turn_index * step_len
            key_block = lax.dynamic_slice_in_dim(query_key_piece, offset, step_len, 1).reshape(
                group_size, step_len, head_count, HEAD
            )
            value_block = lax.dynamic_slice_in_dim(value_piece, offset, step_len, 1).reshape(
                group_size, step_len, head_count, HEAD
            )
            key_pos = true_positions(stretch_order, offset, step_len, stretch_len)
            key_seg = lax.dynamic_slice_in_dim(seg_whole, offset, step_len, 1)
            allowed = (
                (seg_local[:, :, None] == key_seg[:, None, :])
                & (key_pos[None, None, :] <= own_pos[None, :, None])
            )[:, None]
            scores = (
                jnp.einsum(
                    "gqhd,gkhd->ghqk", query_heads, key_block, preferred_element_type=jnp.float32
                )
                * score_scale
            )
            probs = jnp.where(allowed, jnp.exp(scores - log_total[..., None]), 0.0)
            dots = jnp.einsum(
                "gqhd,gkhd->ghqk", grad_heads, value_block, preferred_element_type=jnp.float32
            )
            score_delta = (probs * (dots - delta_heads[..., None])).astype(jnp.bfloat16)
            return running + jnp.einsum(
                "ghqk,gkhd->ghqd", score_delta, key_block, preferred_element_type=jnp.float32
            )

        query_acc = lax.fori_loop(0, count // step_len, query_block_step, head_zeros)
        grad_rows3 = attended_delta.reshape(group_size, stretch_len, model_width)
        query_piece_rows = lax.all_gather(queries, "ctx", axis=1, tiled=True)
        grad_piece = lax.all_gather(grad_rows3, "ctx", axis=1, tiled=True)
        count = query_piece_rows.shape[1]
        key_step_len = piece_size(count)

        def key_block_step(turn_index, running):
            key_acc, value_acc = running
            offset = turn_index * key_step_len
            query_block = lax.dynamic_slice_in_dim(
                query_piece_rows, offset, key_step_len, 1
            ).reshape(group_size, key_step_len, head_count, HEAD)
            grad_block = lax.dynamic_slice_in_dim(grad_piece, offset, key_step_len, 1).reshape(
                group_size, key_step_len, head_count, HEAD
            )
            query_pos = true_positions(stretch_order, offset, key_step_len, stretch_len)
            query_seg = lax.dynamic_slice_in_dim(seg_whole, offset, key_step_len, 1)
            lse_block = lax.dynamic_slice_in_dim(lse_whole, offset, key_step_len, 1).transpose(
                0, 2, 1
            )
            delta_block = lax.dynamic_slice_in_dim(delta_whole, offset, key_step_len, 1).transpose(
                0, 2, 1
            )
            allowed = (
                (query_seg[:, :, None] == seg_local[:, None, :])
                & (own_pos[None, None, :] <= query_pos[None, :, None])
            )[:, None]
            scores = (
                jnp.einsum(
                    "gqhd,gkhd->ghqk", query_block, key_heads, preferred_element_type=jnp.float32
                )
                * score_scale
            )
            probs = jnp.where(allowed, jnp.exp(scores - lse_block[..., None]), 0.0)
            value_acc = value_acc + jnp.einsum(
                "ghqk,gqhd->ghkd",
                probs.astype(jnp.bfloat16),
                grad_block,
                preferred_element_type=jnp.float32,
            )
            dots = jnp.einsum(
                "gqhd,gkhd->ghqk", grad_block, value_heads, preferred_element_type=jnp.float32
            )
            score_delta = (probs * (dots - delta_block[..., None])).astype(jnp.bfloat16)
            key_acc = key_acc + jnp.einsum(
                "ghqk,gqhd->ghkd", score_delta, query_block, preferred_element_type=jnp.float32
            )
            return (key_acc, value_acc)

        key_acc, value_acc = lax.fori_loop(
            0, count // key_step_len, key_block_step, (head_zeros, head_zeros)
        )
        query_delta = (
            (query_acc * score_scale)
            .transpose(0, 2, 1, 3)
            .reshape(row_count, model_width)
            .astype(jnp.bfloat16)
        )
        key_delta = (
            (key_acc * score_scale)
            .transpose(0, 2, 1, 3)
            .reshape(row_count, model_width)
            .astype(jnp.bfloat16)
        )
        value_delta = (
            value_acc.transpose(0, 2, 1, 3).reshape(row_count, model_width).astype(jnp.bfloat16)
        )
        joint_delta = jnp.concatenate([query_delta, key_delta, value_delta], axis=1)
        normed_grad = times_transposed(joint_delta, joint_full)
        first_pull = jax.vjp(
            layer_norm,
            tokens.reshape(row_count, model_width),
            gain_one.astype(jnp.float32),
            shift_one.astype(jnp.float32),
        )[1]
        token_grad, gain_one_grad, shift_one_grad = first_pull(normed_grad)
        input_grad = (middle_grad + token_grad).reshape(group_size, stretch_len, model_width)
        small_terms = (
            gain_one_grad,
            shift_one_grad,
            jnp.sum(query_delta.astype(jnp.float32), axis=0),
            jnp.sum(value_delta.astype(jnp.float32), axis=0),
            jnp.sum(branch_delta.astype(jnp.float32), axis=0),
            gain_two_grad,
            shift_two_grad,
            jnp.sum(expand_delta.astype(jnp.float32), axis=0),
            jnp.sum(tangent_rows.astype(jnp.float32), axis=0),
        )
        factor_pairs = (
            normed.reshape(row_count, model_width),
            joint_delta,
            mixed_rows,
            branch_delta,
            second,
            expand_delta,
            active,
            tangent_rows,
        )
        return (input_grad, small_terms, factor_pairs)

    output_list = []
    input_list = []
    factor_list = []
    small_totals = None
    for micro_index in range(MICRO):
        forward_weights = fetch_weights(local_parts)
        (
            forward_joint_full,
            forward_mixer_full,
            forward_expand_full,
            forward_shrink_full,
            forward_gain_one,
            forward_shift_one,
            forward_qbias_full,
            forward_vbias_full,
            forward_mbias_full,
            forward_gain_two,
            forward_shift_two,
            forward_ebias_full,
            forward_sbias_full,
        ) = forward_weights
        forward_lower = micro_index * group_size
        forward_tokens = inputs[forward_lower : forward_lower + group_size].astype(jnp.float32)
        forward_seg_local = segments[forward_lower : forward_lower + group_size]
        forward_seg_whole = all_segments[forward_lower : forward_lower + group_size]
        forward_normed = layer_norm(
            forward_tokens,
            forward_gain_one.astype(jnp.float32),
            forward_shift_one.astype(jnp.float32),
        ).astype(jnp.bfloat16)
        joint_bias = jnp.concatenate(
            [forward_qbias_full, jnp.zeros_like(forward_qbias_full), forward_vbias_full]
        ).astype(jnp.float32)
        joint_rows = (
            jnp.dot(
                forward_normed.reshape(row_count, model_width),
                forward_joint_full,
                preferred_element_type=jnp.float32,
            )
            + joint_bias
        )
        joint_rows = joint_rows.astype(jnp.bfloat16).reshape(
            group_size, stretch_len, 3 * model_width
        )
        forward_queries = joint_rows[..., :model_width]
        forward_keys_local = joint_rows[..., model_width : 2 * model_width]
        forward_values_local = joint_rows[..., 2 * model_width :]
        forward_query_heads = forward_queries.reshape(group_size, stretch_len, head_count, HEAD)
        start_state = (
            jnp.full((group_size, head_count, stretch_len), masked_score, jnp.float32),
            jnp.zeros((group_size, head_count, stretch_len), jnp.float32),
            jnp.zeros((group_size, head_count, stretch_len, HEAD), jnp.float32),
        )
        forward_key_piece = lax.all_gather(forward_keys_local, "ctx", axis=1, tiled=True)
        forward_value_piece = lax.all_gather(forward_values_local, "ctx", axis=1, tiled=True)
        forward_count = forward_key_piece.shape[1]
        forward_step_len = piece_size(forward_count)

        def forward_block_step(turn_index, state):
            top_score, row_total, accumulated = state
            offset = turn_index * forward_step_len
            key_block = lax.dynamic_slice_in_dim(
                forward_key_piece, offset, forward_step_len, 1
            ).reshape(group_size, forward_step_len, head_count, HEAD)
            value_block = lax.dynamic_slice_in_dim(
                forward_value_piece, offset, forward_step_len, 1
            ).reshape(group_size, forward_step_len, head_count, HEAD)
            key_pos = true_positions(stretch_order, offset, forward_step_len, stretch_len)
            key_seg = lax.dynamic_slice_in_dim(forward_seg_whole, offset, forward_step_len, 1)
            allowed = (
                (forward_seg_local[:, :, None] == key_seg[:, None, :])
                & (key_pos[None, None, :] <= own_pos[None, :, None])
            )[:, None]
            scores = (
                jnp.einsum(
                    "gqhd,gkhd->ghqk",
                    forward_query_heads,
                    key_block,
                    preferred_element_type=jnp.float32,
                )
                * score_scale
            )
            scores = jnp.where(allowed, scores, masked_score)
            new_top = jnp.maximum(top_score, jnp.max(scores, axis=-1))
            weights_now = jnp.where(allowed, jnp.exp(scores - new_top[..., None]), 0.0)
            fade_factor = jnp.exp(top_score - new_top)
            row_total = row_total * fade_factor + jnp.sum(weights_now, axis=-1)
            accumulated = accumulated * fade_factor[..., None] + jnp.einsum(
                "ghqk,gkhd->ghqd",
                weights_now.astype(jnp.bfloat16),
                value_block,
                preferred_element_type=jnp.float32,
            )
            return (new_top, row_total, accumulated)

        top_score, row_total, accumulated = lax.fori_loop(
            0, forward_count // forward_step_len, forward_block_step, start_state
        )
        forward_attended = accumulated / row_total[..., None]
        forward_log_total = top_score + jnp.log(row_total)
        forward_mixed_rows = (
            forward_attended.transpose(0, 2, 1, 3)
            .reshape(row_count, model_width)
            .astype(jnp.bfloat16)
        )
        branch = jnp.dot(
            forward_mixed_rows, forward_mixer_full, preferred_element_type=jnp.float32
        ) + forward_mbias_full.astype(jnp.float32)
        forward_middle = forward_tokens.reshape(row_count, model_width) + branch
        forward_second = layer_norm(
            forward_middle,
            forward_gain_two.astype(jnp.float32),
            forward_shift_two.astype(jnp.float32),
        ).astype(jnp.bfloat16)
        forward_expanded = jnp.dot(
            forward_second, forward_expand_full, preferred_element_type=jnp.float32
        ) + forward_ebias_full.astype(jnp.float32)
        forward_active = jax.nn.gelu(forward_expanded, approximate=True).astype(jnp.bfloat16)
        output = (
            forward_middle
            + jnp.dot(forward_active, forward_shrink_full, preferred_element_type=jnp.float32)
            + forward_sbias_full.astype(jnp.float32)
        )
        forward_kept_values = (
            forward_tokens,
            forward_seg_local,
            forward_seg_whole,
            forward_normed,
            forward_queries,
            forward_keys_local,
            forward_values_local,
            forward_mixed_rows,
            forward_attended,
            forward_log_total,
            forward_middle,
            forward_second,
            forward_expanded,
            forward_active,
        )
        output_now = output.reshape(group_size, stretch_len, model_width).astype(jnp.bfloat16)
        kept_values = forward_kept_values
        backward_weights = fetch_weights(local_parts)
        input_now, small_terms, factor_pairs = backward_micro(
            backward_weights, kept_values, micro_index
        )
        output_list.append(output_now)
        input_list.append(input_now)
        factor_list.append(factor_pairs)
        if small_totals is None:
            small_totals = small_terms
        else:
            small_totals = tuple(
                (total_now + term_now for total_now, term_now in zip(small_totals, small_terms))
            )

    def joined(position):
        return jnp.concatenate([pairs_now[position] for pairs_now in factor_list], axis=0)

    matrices = (
        outer_sum(joined(0), joined(1)),
        outer_sum(joined(2), joined(3)),
        outer_sum(joined(4), joined(5)),
        outer_sum(joined(6), joined(7)),
    )
    reduced = reduce_gradients(matrices, small_totals)
    block_output = jnp.concatenate(output_list, axis=0)
    input_gradient = jnp.concatenate(input_list, axis=0)
    return (
        block_output,
        input_gradient,
        reduced[4],
        reduced[5],
        reduced[0],
        reduced[6],
        reduced[7],
        reduced[1],
        reduced[8],
        reduced[9],
        reduced[10],
        reduced[2],
        reduced[11],
        reduced[3],
        reduced[12],
    )


def solution(mesh):
    in_specs = (
        P("fsdp", "ctx", None),
        P("fsdp", "ctx", None),
        P("fsdp", "ctx"),
        P(),
        P("ctx"),
        P("ctx"),
        P("fsdp", "ctx"),
        P("ctx"),
        P("ctx"),
        P("fsdp", "ctx"),
        P("ctx"),
        P("ctx"),
        P("ctx"),
        P("fsdp", "ctx"),
        P("ctx"),
        P("fsdp", "ctx"),
        P("ctx"),
    )
    out_specs = (
        P("fsdp", "ctx", None),
        P("fsdp", "ctx", None),
        P("ctx"),
        P("ctx"),
        P("fsdp", "ctx"),
        P("ctx"),
        P("ctx"),
        P("fsdp", "ctx"),
        P("ctx"),
        P("ctx"),
        P("ctx"),
        P("fsdp", "ctx"),
        P("ctx"),
        P("fsdp", "ctx"),
        P("ctx"),
    )
    return jax.shard_map(local, mesh=mesh, in_specs=in_specs, out_specs=out_specs, check_vma=False)
```

profile of v0, /device:TPU:0, one launch (start us, length us, event | category | flops | bytes accessed | tf_op | source)
XLA Modules:
  0.0 2576.4 jit_solution(15537170681412599217)
XLA Ops:
  8.0 76.5 %all-gather.49.cloned.1.call-done = bf16[8,600,400]{1,2,0:T(8,128)(2,1)} async-done(((bf16[1,600,400]{1,2,0:T(8,128)(2,1)}), bf16[8,600,400]{1,2,0:T(8,128)(2,1)}) %all-gather.49.cloned.1.call-update) | async-done | bytes 3840016 | tf_op jit(solution)/shard_map/all_gather | solution.py:66
  104.1 35.4 %all-reduce.22 = (bf16[1600]{0:T(1024)(128)(2,1)S(1)}, bf16[1600]{0:T(1024)(128)(2,1)S(1)}, bf16[1600]{0:T(1024)(128)(2,1)S(1)}, bf16[1600]{0:T(1024)(128)(2,1)S...) all-reduce(bf16[1600]{0:T(1024)(128)(2,1)S(1)} %dynamic-update-slic, ...), channel_id=1, replica_groups=mesh['fsdp'=4,'ctx'=8] {'ctx'}, use_global_device_ids=true, to_apply=%add.1 | all-reduce | flops 17600 | bytes 70400
  140.6 54.5 %all-gather.21.cloned.1.call-done = bf16[1600,4800]{1,0:T(8,128)(2,1)} async-done(((bf16[400,4800]{1,0:T(8,128)(2,1)}), bf16[1600,4800]{1,0:T(8,128)(2,1)}) %all-gather.21.cloned.1.call-update) | async-done | bytes 15360016 | tf_op jit(solution)/shard_map/all_gather | solution.py:81
  195.1 11.7 fusion.164
  209.0 11.7 fusion.165
  222.5 20.2 all-gather.27.cloned.1.call-done
  246.2 88.8 %all-gather.51.cloned.1.call-done = bf16[8,800,400]{1,2,0:T(8,128)(2,1)} async-done(((bf16[1,800,400]{1,2,0:T(8,128)(2,1)}), bf16[8,800,400]{1,2,0:T(8,128)(2,1)}) %all-gather.51.cloned.1.call-update) | async-done | bytes 5120016 | tf_op jit(solution)/shard_map/all_gather | solution.py:68
  341.3 10.1 reshape.1695
  351.5 70.7 %all-gather.33.cloned.1.call-done = bf16[1600,1600]{0,1:T(8,128)(2,1)} async-done(((bf16[1600,200]{0,1:T(8,128)(2,1)}), bf16[1600,1600]{0,1:T(8,128)(2,1)}) %all-gather.33.cloned.1.call-update) | async-done | bytes 5120016 | tf_op jit(solution)/shard_map/all_gather | solution.py:69
  422.2 9.5 copy.89
  433.6 17.8 all_gather.60
  452.0 35.6 %all-gather.37.cloned.1.call-done = bf16[1,1024,1600]{1,2,0:T(8,128)(2,1)} async-done(((bf16[1,128,1600]{1,2,0:T(8,128)(2,1)}), bf16[1,1024,1600]{1,2,0:T(8,128)(2,1)}) %all-gather.37.cloned.1.call-update) | async-done | bytes 3276816 | tf_op jit(solution)/shard_map/all_gather | solution.py:454
  487.6 65.0 %all-gather.39.cloned.1.call-done = bf16[1,1024,1600]{1,2,0:T(8,128)(2,1)} async-done(((bf16[1,128,1600]{1,2,0:T(8,128)(2,1)}), bf16[1,1024,1600]{1,2,0:T(8,128)(2,1)}) %all-gather.39.cloned.1.call-update) | async-done | bytes 3276816 | tf_op jit(solution)/shard_map/all_gather | solution.py:455
  552.6 30.4 %while.109 = (s32[]{:T(128)}, f32[1,25,128]{2,1,0:T(8,128)S(1)}, f32[1,25,128]{2,1,0:T(8,128)S(1)}, f32[1,25,128,64]{2,3,1,0:T(8,128)}, s32[1,128]{1,0:T(1,128)S...) while((s32[]{:T(128)}, f32[1,25,128]{2,1,0:T(8,128)S(1)}, ...), condition=%wide.region_16.17_spmd.clone, body=%wide.region_12.16_spmd.clone.sunk | while | flops 441587072 | bytes 58240796 | solution.py:496
  582.9 34.1 %all-gather.23.cloned.1.call-done = bf16[1,1024,1600]{1,2,0:T(8,128)(2,1)} async-done(((bf16[1,128,1600]{1,2,0:T(8,128)(2,1)}), bf16[1,1024,1600]{1,2,0:T(8,128)(2,1)}) %all-gather.23.cloned.1.call-update) | async-done | bytes 3276816 | tf_op jit(solution)/shard_map/all_gather | solution.py:454
  617.0 64.4 %all-gather.25.cloned.1.call-done = bf16[1,1024,1600]{1,2,0:T(8,128)(2,1)} async-done(((bf16[1,128,1600]{1,2,0:T(8,128)(2,1)}), bf16[1,1024,1600]{1,2,0:T(8,128)(2,1)}) %all-gather.25.cloned.1.call-update) | async-done | bytes 3276816 | tf_op jit(solution)/shard_map/all_gather | solution.py:455
  681.4 31.5 %while.108 = (s32[]{:T(128)}, f32[1,25,128]{2,1,0:T(8,128)S(1)}, f32[1,25,128]{2,1,0:T(8,128)S(1)}, f32[1,25,128,64]{2,3,1,0:T(8,128)}, s32[1,128]{1,0:T(1,128)S...) while((s32[]{:T(128)}, f32[1,25,128]{2,1,0:T(8,128)S(1)}, ...), condition=%wide.region_7.8_spmd.clone, body=%wide.region_3.7_spmd.clone.sunk | while | flops 441587072 | bytes 58240796 | solution.py:496
  730.8 122.1 %all-gather.31.cloned.1.call-done = bf16[1600,6400]{1,0:T(8,128)(2,1)} async-done(((bf16[400,6400]{1,0:T(8,128)(2,1)}), bf16[1600,6400]{1,0:T(8,128)(2,1)}) %all-gather.31.cloned.1.call-update) | async-done | bytes 20480016 | tf_op jit(solution)/shard_map/all_gather | solution.py:83
  853.0 13.9 multiply_convert_fusion.12
  876.1 111.7 %all-gather.35.cloned.1.call-done = bf16[6400,1600]{1,0:T(8,128)(2,1)} async-done(((bf16[1600,1600]{1,0:T(8,128)(2,1)}), bf16[6400,1600]{1,0:T(8,128)(2,1)}) %all-gather.35.cloned.1.call-update) | async-done | bytes 20480016 | tf_op jit(solution)/shard_map/all_gather | solution.py:84
  987.8 12.2 convert_reduce_fusion.1
  1000.0 10.3 fusion.296
  1010.3 12.1 convert_reduce_fusion
  1022.4 13.3 multiply_reduce_fusion
  1040.8 33.3 %all_gather.158 = f32[1,1024,25]{1,2,0:T(8,128)} all-gather(f32[1,128,25]{1,2,0:T(8,128)S(1)} %bitcast.658), channel_id=1, replica_groups=mesh['fsdp'=4,'ctx'=8] {'ctx'}, dimensions={1}, use_global_device_ids=true | all-gather | bytes 115200 | tf_op jit(solution)/shard_map/all_gather | solution.py:259
  1074.1 33.4 %all_gather.154 = f32[1,1024,25]{1,2,0:T(8,128)} all-gather(f32[1,128,25]{1,2,0:T(8,128)S(1)} %bitcast.656), channel_id=1, replica_groups=mesh['fsdp'=4,'ctx'=8] {'ctx'}, dimensions={1}, use_global_device_ids=true | all-gather | bytes 115200 | tf_op jit(solution)/shard_map/all_gather | solution.py:259
  1108.7 33.1 %all_gather.160 = f32[1,1024,25]{1,2,0:T(8,128)} all-gather(f32[1,128,25]{1,2,0:T(8,128)S(1)} %bitcast.653), channel_id=1, replica_groups=mesh['fsdp'=4,'ctx'=8] {'ctx'}, dimensions={1}, use_global_device_ids=true | all-gather | bytes 115200 | tf_op jit(solution)/shard_map/all_gather | solution.py:260
  1146.7 29.9 %while.112 = (s32[]{:T(128)}, f32[1,25,128,64]{2,3,1,0:T(8,128)}, s32[1,128]{1,0:T(1,128)S(1)}, s32[1,1024]{1,0:T(1,128)S(1)}, s32[8]{0:T(128)S(1)}, /*index=5*/...) while((s32[]{:T(128)}, f32[1,25,128,64]{2,3,1,0:T(8,128)}, ...), condition=%wide.region_36.37_spmd.clone, body=%wide.region_34.36_spmd.clone.sunk | while | flops 639609472 | bytes 27210504 | solution.py:300
  1178.0 33.1 %all_gather.156 = f32[1,1024,25]{1,2,0:T(8,128)} all-gather(f32[1,128,25]{1,2,0:T(8,128)S(1)} %bitcast.650), channel_id=1, replica_groups=mesh['fsdp'=4,'ctx'=8] {'ctx'}, dimensions={1}, use_global_device_ids=true | all-gather | bytes 115200 | tf_op jit(solution)/shard_map/all_gather | solution.py:260
  1218.0 29.9 %while.110 = (s32[]{:T(128)}, f32[1,25,128,64]{2,3,1,0:T(8,128)}, s32[1,128]{1,0:T(1,128)S(1)}, s32[1,1024]{1,0:T(1,128)S(1)}, s32[8]{0:T(128)S(1)}, /*index=5*/...) while((s32[]{:T(128)}, f32[1,25,128,64]{2,3,1,0:T(8,128)}, ...), condition=%wide.region_24.25_spmd.clone, body=%wide.region_22.24_spmd.clone.sunk | while | flops 639609472 | bytes 33764160 | solution.py:300
  1250.6 40.3 %while.113 = (s32[]{:T(128)}, f32[1,25,128,64]{2,3,1,0:T(8,128)}, f32[1,25,128,64]{2,3,1,0:T(8,128)}, s32[1,1024]{1,0:T(1,128)S(1)}, s32[1,128]{1,0:T(1,128)S(1)...) while((s32[]{:T(128)}, f32[1,25,128,64]{2,3,1,0:T(8,128)}, ...), condition=%wide.region_39.40_spmd.clone, body=%wide.region_37.39_spmd.clone.sunk | while | flops 856287872 | bytes 39896936 | solution.py:350
  1257.1 8.4 fusion.453
  1277.1 8.7 fusion.453
  1295.1 40.5 %while.111 = (s32[]{:T(128)}, f32[1,25,128,64]{2,3,1,0:T(8,128)}, f32[1,25,128,64]{2,3,1,0:T(8,128)}, s32[1,1024]{1,0:T(1,128)S(1)}, s32[1,128]{1,0:T(1,128)S(1)...) while((s32[]{:T(128)}, f32[1,25,128,64]{2,3,1,0:T(8,128)}, ...), condition=%wide.region_27.28_spmd.clone, body=%wide.region_25.27_spmd.clone.sunk | while | flops 856287872 | bytes 39896936 | solution.py:350
  1301.8 8.5 fusion.433
  1321.8 8.6 fusion.433
  1338.4 14.0 convolution_convert_fusion.2
  1354.4 11.6 convolution_convert_fusion.1
  1368.3 9.8 convolution_convert_fusion
  1380.5 308.0 %reduce-scatter.34.cloned.1.call-done = bf16[1600,600]{0,1:T(8,128)(2,1)} async-done(((bf16[1600,4800]{0,1:T(8,128)(2,1)}), bf16[1600,600]{0,1:T(8,128)(2,1)}) %reduce-scatter.34.cloned.1.call-update) | async-done | bytes 1920016
  1692.8 346.3 %reduce-scatter.24.cloned.1.call-done = bf16[1600,800]{0,1:T(8,128)(2,1)} async-done(((bf16[1600,6400]{0,1:T(8,128)(2,1)}), bf16[1600,800]{0,1:T(8,128)(2,1)}) %reduce-scatter.24.cloned.1.call-update) | async-done | bytes 2560016 | tf_op jit(solution)/shard_map/reduce_scatter | solution.py:108
  2046.5 8.8 fusion.211
  2055.4 9.4 fusion.244
  2064.8 360.1 %reduce-scatter.38.cloned.1.call-done = bf16[6400,200]{0,1:T(8,128)(2,1)} async-done(((bf16[6400,1600]{0,1:T(8,128)(2,1)}), bf16[6400,200]{0,1:T(8,128)(2,1)}) %reduce-scatter.38.cloned.1.call-update) | async-done | bytes 2560016
  2430.6 39.3 %all-reduce.21 = (bf16[1600]{0:T(1024)(128)(2,1)S(1)}, bf16[1600]{0:T(1024)(128)(2,1)S(1)}, bf16[1600]{0:T(1024)(128)(2,1)S(1)}, bf16[1600]{0:T(1024)(128)(2,1)S...) all-reduce(bf16[1600]{0:T(1024)(128)(2,1)S(1)} %dynamic-update-slic, ...), channel_id=1, replica_groups=mesh['fsdp'=4,'ctx'=8] {'ctx'}, use_global_device_ids=true, to_apply=%add.8 | all-reduce | flops 20800 | bytes 83200
  2482.2 12.3 fusion.203
  2494.5 13.3 fusion.204
  2528.4 38.4 %reduce-scatter.32.cloned.1.call-done = bf16[1600,200]{1,0:T(8,128)(2,1)} async-done(((bf16[6400,200]{1,0:T(8,128)(2,1)}), bf16[1600,200]{1,0:T(8,128)(2,1)}) %reduce-scatter.32.cloned.1.call-update) | async-done | bytes 640016
  (533 shorter events, 316.3 us)
Async XLA Ops:
  7.2 77.3 %all-gather.49.cloned.1.call-start = ((), (), s32[]{:S(2)}) async-start(), calls=%async_computation.23 | async-start | bytes 4608000 | tf_op jit(solution)/shard_map/all_gather | solution.py:66
  7.9 187.2 %all-gather.21.cloned.1.call-start = ((), (), s32[]{:S(2)}) async-start(), calls=%async_computation.8 | async-start | bytes 19456000 | tf_op jit(solution)/shard_map/all_gather | solution.py:81
  97.3 145.4 %all-gather.27.cloned.1.call-start = ((), (), s32[]{:S(2)}) async-start(), calls=%async_computation.11 | async-start | bytes 1843200 | tf_op jit(solution)/shard_map/all_gather | solution.py:67
  98.9 236.1 %all-gather.51.cloned.1.call-start = ((), (), s32[]{:S(2)}) async-start(), calls=%async_computation.24 | async-start | bytes 6451200 | tf_op jit(solution)/shard_map/all_gather | solution.py:68
  99.5 322.7 %all-gather.33.cloned.1.call-start = ((), (), s32[]{:S(2)}) async-start(), calls=%async_computation.14 | async-start | bytes 5990400 | tf_op jit(solution)/shard_map/all_gather | solution.py:69
  100.1 387.5 %all-gather.37.cloned.1.call-start = ((), (), s32[]{:S(2)}) async-start(), calls=%async_computation.16 | async-start | bytes 3686400 | tf_op jit(solution)/shard_map/all_gather | solution.py:454
  207.9 344.6 %all-gather.39.cloned.1.call-start = ((), (), s32[]{:S(2)}) async-start(), calls=%async_computation.17 | async-start | bytes 3686400 | tf_op jit(solution)/shard_map/all_gather | solution.py:455
  208.7 408.3 %all-gather.23.cloned.1.call-start = ((), (), s32[]{:S(2)}) async-start(), calls=%async_computation.9 | async-start | bytes 3686400 | tf_op jit(solution)/shard_map/all_gather | solution.py:454
  221.7 459.7 %all-gather.25.cloned.1.call-start = ((), (), s32[]{:S(2)}) async-start(), calls=%async_computation.10 | async-start | bytes 3686400 | tf_op jit(solution)/shard_map/all_gather | solution.py:455
  222.4 500.0 %all-gather.29.cloned.1.call-start = ((), (), s32[]{:S(2)}) async-start(), calls=%async_computation.12 | async-start | bytes 6656000 | tf_op jit(solution)/shard_map/all_gather | solution.py:82
  246.2 606.8 %all-gather.31.cloned.1.call-start = ((), (), s32[]{:S(2)}) async-start(), calls=%async_computation.13 | async-start | bytes 25600000 | tf_op jit(solution)/shard_map/all_gather | solution.py:83
  351.5 636.3 %all-gather.35.cloned.1.call-start = ((), (), s32[]{:S(2)}) async-start(), calls=%async_computation.15 | async-start | bytes 26624000 | tf_op jit(solution)/shard_map/all_gather | solution.py:84
  431.7 120.9 %copy-start.5 = (bf16[1,128,1600]{1,2,0:T(8,128)(2,1)S(1)}, bf16[1,128,1600]{1,2,0:T(8,128)(2,1)}, u32[]{:S(2)}) copy-start(bf16[1,128,1600]{1,2,0:T(8,128)(2,1)} %get-tuple-element.2435) | copy-start | bytes 1228804
  431.7 818.9 %all-gather.43.cloned.1.call-start = ((), (), s32[]{:S(2)}) async-start(), calls=%async_computation.19 | async-start | bytes 3686400 | tf_op jit(solution)/shard_map/all_gather | solution.py:302
  451.4 799.2 %all-gather.47.cloned.1.call-start = ((), (), s32[]{:S(2)}) async-start(), calls=%async_computation.22 | async-start | bytes 3686400 | tf_op jit(solution)/shard_map/all_gather | solution.py:303
  727.4 308.4 %copy-start.6 = (f32[128,1600]{0,1:T(8,128)}, f32[128,1600]{0,1:T(8,128)S(1)}, u32[]{:S(2)}) copy-start(f32[128,1600]{0,1:T(8,128)S(1)} %get-tuple-element.2463) | copy-start | bytes 2457604
  730.0 305.7 %copy-start.8 = (f32[128,1600]{0,1:T(8,128)}, f32[128,1600]{0,1:T(8,128)S(1)}, u32[]{:S(2)}) copy-start(f32[128,1600]{0,1:T(8,128)S(1)} %get-tuple-element.2465) | copy-start | bytes 2457604
  730.8 136.0 %copy-start.27 = (bf16[128,1600]{0,1:T(8,128)(2,1)}, bf16[128,1600]{0,1:T(8,128)(2,1)S(1)}, u32[]{:S(2)}) copy-start(bf16[128,1600]{0,1:T(8,128)(2,1)S(1)} %get-tuple-element.2446) | copy-start | bytes 1228804
  730.8 136.0 %copy-start.26 = (bf16[128,1600]{0,1:T(8,128)(2,1)}, bf16[128,1600]{0,1:T(8,128)(2,1)S(1)}, u32[]{:S(2)}) copy-start(bf16[128,1600]{0,1:T(8,128)(2,1)S(1)} %get-tuple-element.2445) | copy-start | bytes 1228804
  870.4 117.4 %copy-start.21 = (bf16[2,128,1600]{1,2,0:T(8,128)(2,1)S(1)}, bf16[2,128,1600]{1,2,0:T(8,128)(2,1)}, u32[]{:S(2)}) copy-start(bf16[2,128,1600]{1,2,0:T(8,128)(2,1)} %param.30) | copy-start | bytes 2457604
  1040.1 255.0 %all-gather.41.cloned.1.call-start = ((), (), s32[]{:S(2)}) async-start(), calls=%async_computation.18 | async-start | bytes 3686400 | tf_op jit(solution)/shard_map/all_gather | solution.py:302
  1040.7 254.4 %all-gather.45.cloned.1.call-start = ((), (), s32[]{:S(2)}) async-start(), calls=%async_computation.21 | async-start | bytes 3686400 | tf_op jit(solution)/shard_map/all_gather | solution.py:303
  1176.6 201.5 %reduce-scatter.36.cloned.1.call-start = ((), (), s32[]{:S(2)}) async-start(), calls=%async_computation.30 | async-start | bytes 5990400
  1250.5 438.0 %reduce-scatter.34.cloned.1.call-start = ((), (), s32[]{:S(2)}) async-start(), calls=%async_computation.29 | async-start | bytes 17971200
  1352.5 686.5 %reduce-scatter.24.cloned.1.call-start = ((), (), s32[]{:S(2)}) async-start(), calls=%async_computation.20 | async-start | bytes 23961600 | tf_op jit(solution)/shard_map/reduce_scatter | solution.py:108
  1366.0 1058.9 %reduce-scatter.38.cloned.1.call-start = ((), (), s32[]{:S(2)}) async-start(), calls=%async_computation.31 | async-start | bytes 23040000
  1378.1 1135.5 %reduce-scatter.28.cloned.1.call-start = ((), (), s32[]{:S(2)}) async-start(), calls=%async_computation.26 | async-start | bytes 1024000
  1380.5 1135.0 %reduce-scatter.26.cloned.1.call-start = ((), (), s32[]{:S(2)}) async-start(), calls=%async_computation.25 | async-start | bytes 2560000
  1692.5 353.1 %copy-start.91 = (bf16[200]{0:T(256)(128)(2,1)S(1)}, bf16[200]{0:T(256)(128)(2,1)}, u32[]{:S(2)}) copy-start(bf16[200]{0:T(256)(128)(2,1)} %param.45) | copy-start | bytes 1204
  1692.6 353.5 %copy-start.61 = (f32[25,64]{1,0:T(8,128)S(1)}, f32[25,64]{1,0:T(8,128)}, u32[]{:S(2)}) copy-start(f32[25,64]{1,0:T(8,128)} %get-tuple-element.2401) | copy-start | bytes 19204
  1692.6 353.5 %copy-start.62 = (f32[25,64]{1,0:T(8,128)S(1)}, f32[25,64]{1,0:T(8,128)}, u32[]{:S(2)}) copy-start(f32[25,64]{1,0:T(8,128)} %get-tuple-element.2403) | copy-start | bytes 19204
  1692.6 353.6 %copy-start.69 = (f32[1600]{0:T(1024)S(1)}, f32[1600]{0:T(1024)}, u32[]{:S(2)}) copy-start(f32[1600]{0:T(1024)} %get-tuple-element.2441) | copy-start | bytes 19204
  1692.6 353.6 %copy-start.70 = (f32[1600]{0:T(1024)S(1)}, f32[1600]{0:T(1024)}, u32[]{:S(2)}) copy-start(f32[1600]{0:T(1024)} %get-tuple-element.2443) | copy-start | bytes 19204
  1692.6 353.6 %copy-start.65 = (f32[1600]{0:T(1024)S(1)}, f32[1600]{0:T(1024)}, u32[]{:S(2)}) copy-start(f32[1600]{0:T(1024)} %get-tuple-element.2198) | copy-start | bytes 19204
  1692.6 353.6 %copy-start.66 = (f32[1600]{0:T(1024)S(1)}, f32[1600]{0:T(1024)}, u32[]{:S(2)}) copy-start(f32[1600]{0:T(1024)} %get-tuple-element.2451) | copy-start | bytes 19204
  1692.6 353.6 %copy-start.63 = (f32[1600]{0:T(1024)S(1)}, f32[1600]{0:T(1024)}, u32[]{:S(2)}) copy-start(f32[1600]{0:T(1024)} %get-tuple-element.2212) | copy-start | bytes 19204
  1692.6 353.6 %copy-start.64 = (f32[1600]{0:T(1024)S(1)}, f32[1600]{0:T(1024)}, u32[]{:S(2)}) copy-start(f32[1600]{0:T(1024)} %get-tuple-element.2449) | copy-start | bytes 19204
  1692.6 353.6 %copy-start.67 = (f32[1600]{0:T(1024)S(1)}, f32[1600]{0:T(1024)}, u32[]{:S(2)}) copy-start(f32[1600]{0:T(1024)} %get-tuple-element.2210) | copy-start | bytes 19204
  1692.7 353.6 %copy-start.68 = (f32[1600]{0:T(1024)S(1)}, f32[1600]{0:T(1024)}, u32[]{:S(2)}) copy-start(f32[1600]{0:T(1024)} %get-tuple-element.2211) | copy-start | bytes 19204
  1692.7 353.6 %copy-start.71 = (f32[6400]{0:T(1024)S(1)}, f32[6400]{0:T(1024)}, u32[]{:S(2)}) copy-start(f32[6400]{0:T(1024)} %get-tuple-element.2470) | copy-start | bytes 76804
  1692.7 353.6 %copy-start.72 = (f32[6400]{0:T(1024)S(1)}, f32[6400]{0:T(1024)}, u32[]{:S(2)}) copy-start(f32[6400]{0:T(1024)} %get-tuple-element.2472) | copy-start | bytes 76804
  1692.7 353.7 %copy-start.50 = (bf16[1,25,128,64]{2,3,1,0:T(8,128)(2,1)S(1)}, bf16[1,25,128,64]{2,3,1,0:T(8,128)(2,1)}, u32[]{:S(2)}) copy-start(bf16[1,25,128,64]{2,3,1,0:T(8,128)(2,1)} %get-tuple-element.2402) | copy-start | bytes 1228804
  1692.7 353.7 %copy-start.52 = (bf16[1,25,128,64]{2,3,1,0:T(8,128)(2,1)S(1)}, bf16[1,25,128,64]{2,3,1,0:T(8,128)(2,1)}, u32[]{:S(2)}) copy-start(bf16[1,25,128,64]{2,3,1,0:T(8,128)(2,1)} %get-tuple-element.2398) | copy-start | bytes 1228804
  1692.7 353.7 %copy-start.53 = (bf16[1,25,128,64]{2,3,1,0:T(8,128)(2,1)S(1)}, bf16[1,25,128,64]{2,3,1,0:T(8,128)(2,1)}, u32[]{:S(2)}) copy-start(bf16[1,25,128,64]{2,3,1,0:T(8,128)(2,1)} %multiply_convert_fusion.14) | copy-start | bytes 1228804
  1692.7 832.9 %reduce-scatter.30.cloned.1.call-start = ((), (), s32[]{:S(2)}) async-start(), calls=%async_computation.27 | async-start | bytes 3584000
  2044.3 522.4 %reduce-scatter.32.cloned.1.call-start = ((), (), s32[]{:S(2)}) async-start(), calls=%async_computation.28 | async-start | bytes 4096000
  2055.3 374.3 %copy-start.32 = (f32[128,1600]{0,1:T(8,128)}, f32[128,1600]{0,1:T(8,128)S(1)}, u32[]{:S(2)}) copy-start(f32[128,1600]{0,1:T(8,128)S(1)} %fusion.211) | copy-start | bytes 2457604
  2064.8 364.9 %copy-start.33 = (f32[128,1600]{0,1:T(8,128)}, f32[128,1600]{0,1:T(8,128)S(1)}, u32[]{:S(2)}) copy-start(f32[128,1600]{0,1:T(8,128)S(1)} %get-tuple-element.2469) | copy-start | bytes 2457604
  (80 other events, 1204.2 us)
Sparse Core Ops, SparseCore 0:
  10.2 74.2 all-gather.48
  97.4 97.6 all-gather.20
  197.8 44.7 all-gather.26
  244.7 90.2 all-gather.50
  337.1 85.0 all-gather.32
  424.1 63.4 all-gather.36
  490.2 62.3 all-gather.38
  554.6 62.3 all-gather.22
  619.0 62.3 all-gather.24
  683.4 39.0 all-gather.28
  724.0 128.8 all-gather.30
  854.4 133.3 all-gather.34
  989.8 64.5 all-gather.42
  1056.3 64.3 all-gather.46
  1122.6 63.6 all-gather.40
  1188.8 62.7 all-gather.44
  1254.9 122.3 reduce-scatter.35
  1379.5 308.9 reduce-scatter.33
  1692.2 346.8 reduce-scatter.23
  2042.4 382.4 reduce-scatter.37
  2427.4 25.9 reduce-scatter.27
  2456.0 31.1 reduce-scatter.25
  2489.7 35.7 reduce-scatter.29
  2528.0 38.6 reduce-scatter.31
where the time goes:
time: 2580 us
  waiting for transfers between devices  1820 us (71%)
  matrix products  334 us (13%)
  blocking collectives  232 us (9%)
  local copies, waits for them, and re-layouts  117 us (5%)
  other arithmetic  56.1 us (2%)
    unnamed x31, waiting for transfers between devices  718 us
    reduce_scatter x1, waiting for transfers between devices, reduce_gradients(): lax.psum_scatter(matrices[2].astype(jnp.bfloat16), 'ctx', scatter_dimensi...  346 us
    all_gather x2, waiting for transfers between devices, local(): lax.all_gather(forward_values_local, 'ctx', axis=1, tiled=True)  129 us
    all_gather x1, waiting for transfers between devices, fetch_weights(): lax.all_gather(spread_out[2], 'fsdp', axis=0, tiled=True)  122 us
    all_gather x1, waiting for transfers between devices, fetch_weights(): lax.all_gather(spread_out[3], 'fsdp', axis=0, tiled=True)  112 us
    all_gather x1, waiting for transfers between devices, fetch_weights(): lax.all_gather(expand_weight, 'ctx', axis=1, tiled=True)  88.8 us
    all_gather x1, waiting for transfers between devices, fetch_weights(): lax.all_gather(joint_weight, 'ctx', axis=1, tiled=True)  76.5 us
    unnamed x2, blocking collectives  74.6 us
  transfers between devices with their start and end apart: 24, of which 17 were waited for; matrix products, arithmetic and copies ran while one was open for 19% of the time, Pallas kernels for 0%

commit v1 on v0

--- a/solution.py
+++ b/solution.py
@@ -1,10 +1,17 @@
+import functools
+
 import jax
 import jax.numpy as jnp
 from jax import lax
+from jax.experimental import pallas as pl
+from jax.experimental.pallas import tpu as pltpu
 from jax.sharding import PartitionSpec as P
 
 HEAD = 64
 MICRO = 2
+LANES = 128
+STRETCH = 128
+TILE = 256
 
 
 epsilon = 1e-05
@@ -584,6 +591,1092 @@
     )
 
 
+def joint_split(rows, parts, heads_each):
+    count, three, width = rows.shape
+    span = heads_each * HEAD
+    slots = slot_width(heads_each)
+    rows = jnp.pad(rows, ((0, 0), (0, 0), (0, parts * span - width)))
+    rows = rows.reshape(count, three, parts, span)
+    rows = jnp.pad(rows, ((0, 0), (0, 0), (0, 0), (0, slots - span)))
+    return rows.transpose(2, 0, 1, 3).reshape(parts, count, three * slots)
+
+
+def joint_join(pieces, heads_each, width):
+    parts, count, wide = pieces.shape
+    span = heads_each * HEAD
+    rows = pieces.reshape(parts, count, 3, wide // 3)[..., :span]
+    rows = rows.transpose(1, 2, 0, 3).reshape(count, 3, parts * span)
+    return rows[..., :width].reshape(count, 3 * width)
+
+
+def slot_width(heads_each):
+    return -(-heads_each * HEAD // LANES) * LANES
+
+
+def attend_prepare(inv_ref, seg_row_ref, seg_col_ref, seg_row, seg_col):
+    for place in range(inv_ref.shape[0]):
+        stored = inv_ref[place]
+        here = pl.ds(place * STRETCH, STRETCH)
+        seg_row[:, here] = seg_row_ref[pl.ds(stored, 1), :]
+        seg_col[here, :] = seg_col_ref[pl.ds(pl.multiple_of(stored * STRETCH, STRETCH), STRETCH), :]
+
+
+def true_rows(inv_ref, source, column):
+    pieces = []
+    for place in range(inv_ref.shape[0]):
+        at_row = pl.multiple_of(inv_ref[place] * STRETCH, STRETCH)
+        pieces.append(source[pl.ds(at_row, STRETCH), pl.ds(column, LANES)])
+    return jnp.concatenate(pieces, axis=0)
+
+
+def store_true(inv_ref, target, first_place, column, rows):
+    for step in range(rows.shape[0] // STRETCH):
+        at_row = pl.multiple_of(inv_ref[first_place + step] * STRETCH, STRETCH)
+        target[pl.ds(at_row, STRETCH), pl.ds(column, LANES)] = rows[
+            step * STRETCH : (step + 1) * STRETCH
+        ]
+
+
+def attend_forward_kernel(
+    inv_ref, seg_row_ref, seg_col_ref, qkv_ref, out_ref, turned_ref, lse_ref,
+    seg_row, seg_col, q_low, q_high, keys, values_turned, acc, tops, sums,
+):
+    pair = pl.program_id(0)
+    slots = out_ref.shape[1]
+    scale = HEAD ** (-0.5)
+
+    @pl.when(pair == 0)
+    def _():
+        attend_prepare(inv_ref, seg_row_ref, seg_col_ref, seg_row, seg_col)
+
+    column = pl.multiple_of(pair * LANES, LANES)
+    queries = true_rows(inv_ref, qkv_ref, column) * jnp.bfloat16(scale)
+    low_half = lax.broadcasted_iota(jnp.int32, queries.shape, 1) < HEAD
+    q_low[...] = jnp.where(low_half, queries, jnp.zeros_like(queries))
+    q_high[...] = jnp.where(low_half, jnp.zeros_like(queries), queries)
+    keys[...] = true_rows(inv_ref, qkv_ref, slots + column)
+    values = true_rows(inv_ref, qkv_ref, 2 * slots + column)
+    values_turned[...] = values.astype(jnp.float32).T.astype(jnp.bfloat16)
+    halves = (q_low, q_high)
+
+    def one_block(q_block, k_block, first):
+        q_at = pl.ds(pl.multiple_of(q_block * TILE, TILE), TILE)
+        k_at = pl.ds(pl.multiple_of(k_block * TILE, TILE), TILE)
+        same = seg_col[k_at, :] == seg_row[:, q_at]
+        if first:
+            same = same & (
+                lax.broadcasted_iota(jnp.int32, (TILE, TILE), 0)
+                <= lax.broadcasted_iota(jnp.int32, (TILE, TILE), 1)
+            )
+        for half in range(2):
+            dims = pl.ds(half * HEAD, HEAD)
+            scores = times_transposed(keys[k_at, :], halves[half][q_at, :])
+            scores = jnp.where(same, scores, masked_score)
+            top = jnp.max(scores, axis=0, keepdims=True)
+            if not first:
+                old_top = tops[half]
+                top = jnp.maximum(old_top, top)
+            weights = jnp.exp(scores - top)
+            total = jnp.sum(weights, axis=0, keepdims=True)
+            part = jnp.dot(
+                values_turned[dims, k_at],
+                weights.astype(jnp.bfloat16),
+                preferred_element_type=jnp.float32,
+            )
+            if not first:
+                fade = jnp.exp(old_top - top)
+                total = total + sums[half] * fade
+                part = part + acc[dims, :] * fade
+            tops[half] = top
+            sums[half] = total
+            acc[dims, :] = part
+
+    @pl.loop(0, qkv_ref.shape[0] // TILE)
+    def _(q_block):
+        one_block(q_block, q_block, True)
+
+        @pl.loop(0, q_block)
+        def _(k_block):
+            one_block(q_block, k_block, False)
+
+        q_at = pl.ds(pl.multiple_of(q_block * TILE, TILE), TILE)
+        for half in range(2):
+            dims = pl.ds(half * HEAD, HEAD)
+            acc[dims, :] = acc[dims, :] / sums[half]
+            lse_ref[0, pl.ds(half, 1), q_at] = tops[half] + jnp.log(sums[half])
+        turned_ref[0, :, q_at] = acc[...]
+        store_true(
+            inv_ref, out_ref, q_block * (TILE // STRETCH), column, acc[...].T.astype(jnp.bfloat16)
+        )
+
+
+def attend_backward_kernel(
+    inv_ref, seg_row_ref, seg_col_ref, qkv_ref, grad_ref, turned_ref, lse_ref, out_ref,
+    seg_row, seg_col, q_low, q_high, keys, keys_turned, values, g_low, g_high,
+    query_acc, key_acc, value_acc, corrections,
+):
+    pair = pl.program_id(0)
+    slots = grad_ref.shape[1]
+    scale = HEAD ** (-0.5)
+
+    @pl.when(pair == 0)
+    def _():
+        attend_prepare(inv_ref, seg_row_ref, seg_col_ref, seg_row, seg_col)
+
+    column = pl.multiple_of(pair * LANES, LANES)
+    queries = true_rows(inv_ref, qkv_ref, column) * jnp.bfloat16(scale)
+    low_half = lax.broadcasted_iota(jnp.int32, queries.shape, 1) < HEAD
+    zeros = jnp.zeros_like(queries)
+    q_low[...] = jnp.where(low_half, queries, zeros)
+    q_high[...] = jnp.where(low_half, zeros, queries)
+    grads = true_rows(inv_ref, grad_ref, column)
+    g_low[...] = jnp.where(low_half, grads, zeros)
+    g_high[...] = jnp.where(low_half, zeros, grads)
+    product = grads.astype(jnp.float32).T * turned_ref[0]
+    corrections[0] = jnp.sum(product[:HEAD], axis=0, keepdims=True)
+    corrections[1] = jnp.sum(product[HEAD:], axis=0, keepdims=True)
+    keys_now = true_rows(inv_ref, qkv_ref, slots + column)
+    keys[...] = keys_now
+    keys_turned[...] = keys_now.astype(jnp.float32).T.astype(jnp.bfloat16)
+    values[...] = true_rows(inv_ref, qkv_ref, 2 * slots + column)
+    key_acc[...] = jnp.zeros_like(key_acc)
+    value_acc[...] = jnp.zeros_like(value_acc)
+    q_halves = (q_low, q_high)
+    g_halves = (g_low, g_high)
+
+    def one_block(q_block, k_block, first):
+        q_at = pl.ds(pl.multiple_of(q_block * TILE, TILE), TILE)
+        k_at = pl.ds(pl.multiple_of(k_block * TILE, TILE), TILE)
+        same = seg_col[k_at, :] == seg_row[:, q_at]
+        if first:
+            same = same & (
+                lax.broadcasted_iota(jnp.int32, (TILE, TILE), 0)
+                <= lax.broadcasted_iota(jnp.int32, (TILE, TILE), 1)
+            )
+        value_sum = value_acc[k_at, :]
+        key_sum = key_acc[k_at, :]
+        for half in range(2):
+            dims = pl.ds(half * HEAD, HEAD)
+            query_rows = q_halves[half][q_at, :]
+            grad_rows = g_halves[half][q_at, :]
+            scores = times_transposed(keys[k_at, :], query_rows)
+            lse = lse_ref[0, pl.ds(half, 1), q_at]
+            probs = jnp.exp(jnp.where(same, scores - lse, masked_score))
+            dots = times_transposed(values[k_at, :], grad_rows)
+            delta = (probs * (dots - corrections[half, :, q_at])).astype(jnp.bfloat16)
+            value_sum = value_sum + jnp.dot(
+                probs.astype(jnp.bfloat16), grad_rows, preferred_element_type=jnp.float32
+            )
+            key_sum = key_sum + jnp.dot(delta, query_rows, preferred_element_type=jnp.float32)
+            part = jnp.dot(keys_turned[dims, k_at], delta, preferred_element_type=jnp.float32)
+            if first:
+                query_acc[dims, :] = part
+            else:
+                query_acc[dims, :] += part
+        value_acc[k_at, :] = value_sum
+        key_acc[k_at, :] = key_sum
+
+    @pl.loop(0, qkv_ref.shape[0] // TILE)
+    def _(q_block):
+        one_block(q_block, q_block, True)
+
+        @pl.loop(0, q_block)
+        def _(k_block):
+            one_block(q_block, k_block, False)
+
+        store_true(
+            inv_ref,
+            out_ref,
+            q_block * (TILE // STRETCH),
+            column,
+            (query_acc[...].T * scale).astype(jnp.bfloat16),
+        )
+
+    store_true(inv_ref, out_ref, 0, slots + column, key_acc[...].astype(jnp.bfloat16))
+    store_true(inv_ref, out_ref, 0, 2 * slots + column, value_acc[...].astype(jnp.bfloat16))
+
+
+def whole_block(array):
+    return pl.BlockSpec(array.shape, lambda *_, n=array.ndim: (0,) * n)
+
+
+def attend_forward(inverse, seg_blocks, qkv):
+    rows, wide = qkv.shape
+    slots = wide // 3
+    pairs = slots // LANES
+    seg_col = seg_blocks.reshape(rows, 1)
+    outs = (
+        jax.ShapeDtypeStruct((rows, slots), jnp.bfloat16),
+        jax.ShapeDtypeStruct((pairs, LANES, rows), jnp.float32),
+        jax.ShapeDtypeStruct((pairs, 2, rows), jnp.float32),
+    )
+    low = jnp.bfloat16
+    return pl.pallas_call(
+        attend_forward_kernel,
+        grid_spec=pltpu.PrefetchScalarGridSpec(
+            num_scalar_prefetch=1,
+            grid=(pairs,),
+            in_specs=[whole_block(seg_blocks), whole_block(seg_col), whole_block(qkv)],
+            out_specs=[
+                whole_block(outs[0]),
+                pl.BlockSpec((1, LANES, rows), lambda p, *_: (p, 0, 0)),
+                pl.BlockSpec((1, 2, rows), lambda p, *_: (p, 0, 0)),
+            ],
+            scratch_shapes=[
+                pltpu.VMEM((1, rows), jnp.int32),
+                pltpu.VMEM((rows, 1), jnp.int32),
+                pltpu.VMEM((rows, LANES), low),
+                pltpu.VMEM((rows, LANES), low),
+                pltpu.VMEM((rows, LANES), low),
+                pltpu.VMEM((LANES, rows), low),
+                pltpu.VMEM((LANES, TILE), jnp.float32),
+                pltpu.VMEM((2, 1, TILE), jnp.float32),
+                pltpu.VMEM((2, 1, TILE), jnp.float32),
+            ],
+        ),
+        out_shape=outs,
+        name="attend_forward",
+    )(inverse, seg_blocks, seg_col, qkv)
+
+
+def attend_backward(inverse, seg_blocks, qkv, grads, turned, lse):
+    rows, wide = qkv.shape
+    slots = wide // 3
+    pairs = slots // LANES
+    seg_col = seg_blocks.reshape(rows, 1)
+    out = jax.ShapeDtypeStruct((rows, wide), jnp.bfloat16)
+    low = jnp.bfloat16
+    return pl.pallas_call(
+        attend_backward_kernel,
+        grid_spec=pltpu.PrefetchScalarGridSpec(
+            num_scalar_prefetch=1,
+            grid=(pairs,),
+            in_specs=[
+                whole_block(seg_blocks),
+                whole_block(seg_col),
+                whole_block(qkv),
+                whole_block(grads),
+                pl.BlockSpec((1, LANES, rows), lambda p, *_: (p, 0, 0)),
+                pl.BlockSpec((1, 2, rows), lambda p, *_: (p, 0, 0)),
+            ],
+            out_specs=whole_block(out),
+            scratch_shapes=[
+                pltpu.VMEM((1, rows), jnp.int32),
+                pltpu.VMEM((rows, 1), jnp.int32),
+                pltpu.VMEM((rows, LANES), low),
+                pltpu.VMEM((rows, LANES), low),
+                pltpu.VMEM((rows, LANES), low),
+                pltpu.VMEM((LANES, rows), low),
+                pltpu.VMEM((rows, LANES), low),
+                pltpu.VMEM((rows, LANES), low),
+                pltpu.VMEM((rows, LANES), low),
+                pltpu.VMEM((LANES, TILE), jnp.float32),
+                pltpu.VMEM((rows, LANES), jnp.float32),
+                pltpu.VMEM((rows, LANES), jnp.float32),
+                pltpu.VMEM((2, 1, rows), jnp.float32),
+            ],
+        ),
+        out_shape=out,
+        name="attend_backward",
+    )(inverse, seg_blocks, seg_col, qkv, grads, turned, lse)
+
+
+def normalize(rows):
+    center = rows - jnp.mean(rows, axis=-1, keepdims=True)
+    spread = jnp.mean(center * center, axis=-1, keepdims=True)
+    inverse = lax.rsqrt(spread + epsilon)
+    return center * inverse, inverse
+
+
+def normalize_back(grads, gain, unit, inverse):
+    pulled = grads * gain
+    return inverse * (
+        pulled
+        - jnp.mean(pulled, axis=-1, keepdims=True)
+        - unit * jnp.mean(pulled * unit, axis=-1, keepdims=True)
+    )
+
+
+def gelu_parts(value):
+    root = 0.7978845608028654
+    inner = root * (value + 0.044715 * value * value * value)
+    bend = jnp.tanh(inner)
+    slope = 0.5 * (1.0 + bend) + 0.5 * value * (1.0 - bend * bend) * root * (
+        1.0 + 3 * 0.044715 * value * value
+    )
+    return 0.5 * value * (1.0 + bend), slope
+
+
+def mesh_copy(source, target, send, receive, device):
+    return pltpu.make_async_remote_copy(
+        src_ref=source,
+        dst_ref=target,
+        send_sem=send,
+        recv_sem=receive,
+        device_id=device,
+        device_id_type=pl.DeviceIdType.MESH,
+    )
+
+
+def greet(devices):
+    barrier = pltpu.get_barrier_semaphore()
+    for device in devices:
+        pl.semaphore_signal(
+            barrier, inc=1, device_id=device, device_id_type=pl.DeviceIdType.MESH
+        )
+    pl.semaphore_wait(barrier, len(devices))
+
+
+def fsdp_places():
+    shard = lax.axis_index("fsdp")
+    partner = shard + 1 - 2 * (shard % 2)
+    return shard, partner, (shard + 2) % 4, (partner + 2) % 4
+
+
+def ring_places(nc):
+    place = lax.axis_index("ctx")
+    z, y = place // 2, place % 2
+    spot = z * (1 - y) + (nc - 1 - z) * y
+
+    def holder(at):
+        at = (at + nc) % nc
+        side = at // (nc // 2)
+        return (1 - side) * 2 * at + side * (2 * (nc - 1 - at) + 1)
+
+    return spot, holder
+
+
+def chunks_of(rows, count):
+    step = -(-rows // count // 16) * 16
+    return [(at, min(step, rows - at)) for at in range(0, rows, step)]
+
+
+class FsdpGather:
+    SEMS = 7
+
+    def __init__(self, own, out, sems, parts=4):
+        self.own, self.out, self.sems = own, out, sems
+        self.shard, self.partner, self.cross, self.corner = fsdp_places()
+        self.place = lax.axis_index("ctx")
+        self.chunks = chunks_of(own.shape[0], parts)
+
+    def peers(self):
+        return [(self.partner, self.place), (self.cross, self.place)]
+
+    def copy(self, kind, k):
+        at, size = self.chunks[k]
+        rows = pl.ds(at, size)
+        if kind == "own":
+            return pltpu.make_async_copy(
+                self.own.at[rows], self.out.at[self.shard, rows], self.sems.at[6, k]
+            )
+        if kind == "across":
+            source, slot, device, sem = self.own.at[rows], self.shard, self.cross, 0
+        elif kind == "beside":
+            source, slot, device, sem = self.own.at[rows], self.shard, self.partner, 2
+        else:
+            slot, device, sem = self.cross, self.partner, 4
+            source = self.out.at[slot, rows]
+        return mesh_copy(
+            source,
+            self.out.at[slot, rows],
+            self.sems.at[sem, k],
+            self.sems.at[sem + 1, k],
+            (device, self.place),
+        )
+
+    def begin(self):
+        for kind in ("across", "beside", "own"):
+            for k in range(len(self.chunks)):
+                self.copy(kind, k).start()
+
+    def pass_on(self):
+        for k in range(len(self.chunks)):
+            self.copy("across", k).wait_recv()
+            self.copy("on", k).start()
+
+    def finish(self):
+        for k in range(len(self.chunks)):
+            self.copy("across", k).wait_send()
+            self.copy("beside", k).wait()
+            self.copy("on", k).wait()
+            self.copy("own", k).wait()
+
+
+class RingGather:
+    def __init__(self, nc, own, out, sems):
+        self.nc, self.own, self.out, self.sems = nc, own, out, sems
+        self.spot, self.holder = ring_places(nc)
+        self.shard = lax.axis_index("fsdp")
+        rows = own.shape[0]
+        self.half = rows // 2 // 8 * 8
+        self.rows = rows
+
+    def peers(self):
+        return [(self.shard, self.holder(self.spot + way)) for way in (1, -1)]
+
+    def copy(self, way, step):
+        origin = self.holder(self.spot - way * (step - 1))
+        rows = pl.ds(0, self.rows)
+        if step == self.nc // 2:
+            rows = pl.ds(0, self.half) if way == 1 else pl.ds(self.half, self.rows - self.half)
+        source = self.own.at[rows] if step == 1 else self.out.at[origin, rows]
+        side = 0 if way == 1 else 2
+        return mesh_copy(
+            source,
+            self.out.at[origin, rows],
+            self.sems.at[side, step - 1],
+            self.sems.at[side + 1, step - 1],
+            (self.shard, self.holder(self.spot + way)),
+        )
+
+    def keep(self):
+        return pltpu.make_async_copy(
+            self.own, self.out.at[lax.axis_index("ctx")], self.sems.at[4, 0]
+        )
+
+    def begin(self):
+        for way in (1, -1):
+            self.copy(way, 1).start()
+        self.keep().start()
+
+    def advance(self, step):
+        for way in (1, -1):
+            self.copy(way, step - 1).wait_recv()
+            self.copy(way, step).start()
+
+    def finish(self):
+        last = self.nc // 2
+        for way in (1, -1):
+            for step in range(1, last + 1):
+                self.copy(way, step).wait_send()
+            self.copy(way, last).wait_recv()
+        self.keep().wait()
+
+
+def startup_kernel(nc, ring_count, row_count, *refs):
+    total = ring_count + row_count
+    ins, outs, sems = refs[:total], refs[total : 2 * total], refs[2 * total :]
+    rings = [RingGather(nc, ins[k], outs[k], sems[k]) for k in range(ring_count)]
+    sides = [FsdpGather(ins[k], outs[k], sems[k]) for k in range(ring_count, total)]
+    greet(rings[0].peers() + (sides[0].peers() if sides else []))
+    for ring in rings:
+        ring.begin()
+    for side in sides:
+        side.begin()
+    for step in range(2, nc // 2 + 1):
+        if step - 2 < len(sides):
+            sides[step - 2].pass_on()
+        for ring in rings:
+            ring.advance(step)
+    for side in sides:
+        side.finish()
+    for ring in rings:
+        ring.finish()
+
+
+def gather_fsdp_kernel(own_ref, out_ref, sems):
+    side = FsdpGather(own_ref, out_ref, sems)
+    greet(side.peers())
+    side.begin()
+    side.pass_on()
+    side.finish()
+
+
+def add_rows(target, source, rows):
+    first, size = rows
+    step = 16 if size % 16 == 0 else 8
+
+    @pl.loop(0, size // step)
+    def _(turn):
+        at = pl.ds(pl.multiple_of(first + turn * step, 8), step)
+        target[at] = (target[at].astype(jnp.float32) + source[at].astype(jnp.float32)).astype(
+            target.dtype
+        )
+
+
+def set_rows(target, source, rows):
+    first, size = rows
+    step = 16 if size % 16 == 0 else 8
+
+    @pl.loop(0, size // step)
+    def _(turn):
+        at = pl.ds(pl.multiple_of(first + turn * step, 8), step)
+        target[at] = source[at]
+
+
+def scatter_fsdp_kernel(part_ref, out_ref, first_in, own_in, chip_sum, across_in, sems):
+    shard, partner, cross, corner = fsdp_places()
+    place = lax.axis_index("ctx")
+    greet([(partner, place), (cross, place)])
+    chunks = chunks_of(out_ref.shape[0], 4)
+
+    def copy(kind, k):
+        at, size = chunks[k]
+        rows = pl.ds(at, size)
+        if kind == 0:
+            source, target, device = part_ref.at[corner, rows], first_in, partner
+        elif kind == 1:
+            source, target, device = part_ref.at[partner, rows], own_in, partner
+        else:
+            source, target, device = chip_sum.at[rows], across_in, cross
+        return mesh_copy(
+            source,
+            target.at[rows],
+            sems.at[2 * kind, k],
+            sems.at[2 * kind + 1, k],
+            (device, place),
+        )
+
+    for kind in range(2):
+        for k in range(len(chunks)):
+            copy(kind, k).start()
+    for k, (at, size) in enumerate(chunks):
+        copy(0, k).wait_recv()
+
+        @pl.loop(0, size // 16)
+        def _(turn):
+            rows = pl.ds(pl.multiple_of(at + turn * 16, 16), 16)
+            chip_sum[rows] = (
+                part_ref[cross, rows].astype(jnp.float32) + first_in[rows].astype(jnp.float32)
+            ).astype(chip_sum.dtype)
+
+        copy(2, k).start()
+    for k, (at, size) in enumerate(chunks):
+        copy(1, k).wait_recv()
+        copy(2, k).wait_recv()
+
+        @pl.loop(0, size // 16)
+        def _(turn):
+            rows = pl.ds(pl.multiple_of(at + turn * 16, 16), 16)
+            out_ref[rows] = (
+                part_ref[shard, rows].astype(jnp.float32)
+                + own_in[rows].astype(jnp.float32)
+                + across_in[rows].astype(jnp.float32)
+            )
+
+    for kind in range(3):
+        for k in range(len(chunks)):
+            copy(kind, k).wait_send()
+
+
+class RingScatter:
+    def __init__(self, nc, mine, out, right, left, sems):
+        self.nc, self.mine, self.out, self.sems = nc, mine, out, sems
+        self.inbox = {1: right, -1: left}
+        self.spot, self.holder = ring_places(nc)
+        self.shard = lax.axis_index("fsdp")
+        self.rows = out.shape[0]
+        self.half = self.rows // 2 // 8 * 8
+
+    def peers(self):
+        return [(self.shard, self.holder(self.spot + way)) for way in (1, -1)]
+
+    def copy(self, way, step):
+        inbox = self.inbox[way]
+        rows = pl.ds(0, self.rows)
+        if step == 1:
+            rows = pl.ds(0, self.half) if way == 1 else pl.ds(self.half, self.rows - self.half)
+            source = self.mine.at[self.holder(self.spot + self.nc // 2), rows]
+        else:
+            source = inbox.at[step - 2, rows]
+        side = 0 if way == 1 else 2
+        return mesh_copy(
+            source,
+            inbox.at[step - 1, rows],
+            self.sems.at[side, step - 1],
+            self.sems.at[side + 1, step - 1],
+            (self.shard, self.holder(self.spot + way)),
+        )
+
+    def begin(self):
+        for way in (1, -1):
+            self.copy(way, 1).start()
+
+    def advance(self, step):
+        for way in (1, -1):
+            self.copy(way, step - 1).wait_recv()
+            box = self.inbox[way].at[step - 2]
+            mine = self.mine.at[self.holder(self.spot + way * (self.nc // 2 + 1 - step))]
+            if step == 2:
+                low, high = (0, self.half), (self.half, self.rows - self.half)
+                got, rest = (low, high) if way == 1 else (high, low)
+                add_rows(box, mine, got)
+                set_rows(box, mine, rest)
+            else:
+                add_rows(box, mine, (0, self.rows))
+            self.copy(way, step).start()
+
+    def finish(self):
+        last = self.nc // 2
+        for way in (1, -1):
+            self.copy(way, last).wait_recv()
+        right, left = self.inbox[1].at[last - 1], self.inbox[-1].at[last - 1]
+        mine = self.mine.at[lax.axis_index("ctx")]
+        step = 16 if self.rows % 16 == 0 else 8
+
+        @pl.loop(0, self.rows // step)
+        def _(turn):
+            at = pl.ds(pl.multiple_of(turn * step, 8), step)
+            self.out[at] = (
+                mine[at].astype(jnp.float32)
+                + right[at].astype(jnp.float32)
+                + left[at].astype(jnp.float32)
+            ).astype(self.out.dtype)
+
+        for way in (1, -1):
+            for step in range(1, last + 1):
+                self.copy(way, step).wait_send()
+
+
+def scatter_ctx_kernel(nc, count, *refs):
+    ins, outs, rest = refs[:count], refs[count : 2 * count], refs[2 * count :]
+    rings = [
+        RingScatter(nc, ins[k], outs[k], rest[3 * k], rest[3 * k + 1], rest[3 * k + 2])
+        for k in range(count)
+    ]
+    greet(rings[0].peers())
+    for ring in rings:
+        ring.begin()
+    for step in range(2, nc // 2 + 1):
+        for ring in rings:
+            ring.advance(step)
+    for ring in rings:
+        ring.finish()
+
+
+def trade_kernel(axes, sizes, *refs):
+    count = len(axes)
+    ins, outs, sems = refs[:count], refs[count : 2 * count], refs[2 * count :]
+    place = {"fsdp": lax.axis_index("fsdp"), "ctx": lax.axis_index("ctx")}
+
+    def device(axis, at):
+        return (at, place["ctx"]) if axis == "fsdp" else (place["fsdp"], at)
+
+    peers = []
+    for axis in sorted(set(axes)):
+        for k in range(1, sizes[axis]):
+            peers.append(device(axis, (place[axis] + k) % sizes[axis]))
+    greet(peers)
+    copies, stays = [], []
+    for j in range(count):
+        axis = axes[j]
+        me = place[axis]
+        stay = pltpu.make_async_copy(ins[j].at[me], outs[j].at[me], sems[j].at[2, 0])
+        stay.start()
+        stays.append(stay)
+        for k in range(1, sizes[axis]):
+            other = (me + k) % sizes[axis]
+            copy = mesh_copy(
+                ins[j].at[other],
+                outs[j].at[me],
+                sems[j].at[0, k],
+                sems[j].at[1, k],
+                device(axis, other),
+            )
+            copy.start()
+            copies.append(copy)
+    for copy in copies:
+        copy.wait()
+    for stay in stays:
+        stay.wait()
+
+
+def in_vmem():
+    return pl.BlockSpec(memory_space=pltpu.VMEM)
+
+
+def in_place():
+    return pl.BlockSpec(memory_space=pl.ANY)
+
+
+def widen(pieces):
+    return jnp.pad(pieces, ((0, 0),) * (pieces.ndim - 1) + ((0, -pieces.shape[-1] % LANES),))
+
+
+class Net:
+    def __init__(self, nf, nc):
+        self.nf, self.nc = nf, nc
+        self.each = nc // nf
+        self.ids = {}
+
+    def call(self, kernel, key, outs, ins, in_specs, out_specs, scratch, name):
+        ident = self.ids.setdefault(key, len(self.ids))
+        return pl.pallas_call(
+            kernel,
+            out_shape=outs,
+            in_specs=in_specs,
+            out_specs=out_specs,
+            scratch_shapes=scratch,
+            compiler_params=pltpu.CompilerParams(
+                collective_id=ident, has_side_effects=True, vmem_limit_bytes=60 << 20
+            ),
+            name=name,
+        )(*ins)
+
+    def to_column(self, f, c, i):
+        return 2 * (c // 2 % 2) + c // 4, 2 * (2 * (f % 2) + i) + f // 2, c % 2
+
+    def to_origin(self, f, c, j):
+        return 2 * (c % 2) + c // 4, 2 * (2 * (f % 2) + f // 2) + j, c // 2 % 2
+
+    def blocks_in_order(self):
+        return [self.to_origin(k // 2, 0, k % 2)[1] for k in range(self.nc)]
+
+    def sequence_of(self, place):
+        return self.each * (2 * (place % 2) + place // 4) + place // 2 % 2
+
+    def swap_blocks(self, blocks, move):
+        place = lax.axis_index("ctx")
+        out_slot = move(0, place, 0)[2]
+        got = []
+        for turn in range(self.each):
+            slot = (out_slot + turn) % self.each
+            piece = lax.dynamic_index_in_dim(blocks, slot, 0, keepdims=False)
+            pairs = []
+            for f in range(self.nf):
+                for c in range(self.nc):
+                    there = move(f, c, (move(f, c, 0)[2] + turn) % self.each)
+                    pairs.append((f * self.nc + c, there[0] * self.nc + there[1]))
+            got.append(lax.ppermute(piece, ("fsdp", "ctx"), pairs))
+        back = self.to_origin if move == self.to_column else self.to_column
+        own_slot = back(0, place, 0)[2]
+        order = (own_slot - jnp.arange(self.each)) % self.each
+        return jnp.take(jnp.stack(got), order, axis=0)
+
+    def trade(self, arrays, axes):
+        sizes = {"fsdp": self.nf, "ctx": self.nc}
+        extents = [a.shape[-1] for a in arrays]
+        arrays = [widen(a) for a in arrays]
+        key = ("trade",) + tuple((a.shape, x) for a, x in zip(arrays, axes))
+        outs = tuple(jax.ShapeDtypeStruct(a.shape, a.dtype) for a in arrays)
+        count = len(arrays)
+        got = self.call(
+            functools.partial(trade_kernel, tuple(axes), sizes),
+            key, outs, arrays, [in_vmem()] * count, [in_place()] * count,
+            [pltpu.SemaphoreType.DMA((3, sizes[x])) for x in axes],
+            "trade",
+        )
+        return [whole[..., :extent] for whole, extent in zip(got, extents)]
+
+    def trade_fsdp(self, pieces):
+        return self.trade([pieces], ["fsdp"])[0]
+
+    def trade_ctx(self, pieces):
+        return self.trade([pieces], ["ctx"])[0]
+
+    def startup(self, blocks, rows):
+        arrays = list(blocks) + list(rows)
+        outs = [jax.ShapeDtypeStruct((self.nc,) + a.shape, a.dtype) for a in blocks]
+        outs += [jax.ShapeDtypeStruct((self.nf,) + a.shape, a.dtype) for a in rows]
+        sems = [pltpu.SemaphoreType.DMA((5, self.nc // 2)) for _ in blocks]
+        sems += [pltpu.SemaphoreType.DMA((FsdpGather.SEMS, 8)) for _ in rows]
+        count = len(arrays)
+        key = ("startup",) + tuple(a.shape for a in arrays)
+        return self.call(
+            functools.partial(startup_kernel, self.nc, len(blocks), len(rows)),
+            key, tuple(outs), arrays, [in_vmem()] * count, [in_place()] * count, sems, "startup",
+        )
+
+    def gather_ctx(self, block):
+        return lax.all_gather(block, "ctx", axis=0)
+
+    def scatter_ctx(self, blocks):
+        return lax.psum_scatter(blocks, "ctx", scatter_dimension=0)
+
+    def ring_scatter(self, arrays):
+        outs, scratch = [], []
+        for a in arrays:
+            outs.append(jax.ShapeDtypeStruct(a.shape[1:], a.dtype))
+            box = pltpu.VMEM((self.nc // 2,) + a.shape[1:], a.dtype)
+            scratch += [box, box, pltpu.SemaphoreType.DMA((4, self.nc // 2))]
+        count = len(arrays)
+        key = ("ring",) + tuple(a.shape for a in arrays)
+        return self.call(
+            functools.partial(scatter_ctx_kernel, self.nc, count),
+            key, tuple(outs), arrays, [in_vmem()] * count, [in_vmem()] * count, scratch,
+            "ring_scatter",
+        )
+
+    def gather_fsdp(self, rows):
+        out = self.call(
+            gather_fsdp_kernel,
+            ("gather", rows.shape),
+            jax.ShapeDtypeStruct((self.nf,) + rows.shape, rows.dtype),
+            [rows], [in_vmem()], in_place(),
+            [pltpu.SemaphoreType.DMA((FsdpGather.SEMS, 8))],
+            "gather_fsdp",
+        )
+        return out.reshape((-1,) + rows.shape[1:])
+
+    def scatter_fsdp(self, rows):
+        count = rows.shape[0] // self.nf
+        block = (count,) + rows.shape[1:]
+        box = pltpu.VMEM(block, rows.dtype)
+        return self.call(
+            scatter_fsdp_kernel,
+            ("scatter", rows.shape),
+            jax.ShapeDtypeStruct(block, jnp.float32),
+            [rows.reshape((self.nf,) + block)], [in_vmem()], in_vmem(),
+            [box, box, box, box, pltpu.SemaphoreType.DMA((6, 8))],
+            "scatter_fsdp",
+        )
+
+
+def local_fast(
+    net,
+    inputs,
+    cotangent,
+    segments,
+    stretch_order,
+    prenorm_gain,
+    prenorm_shift,
+    joint_weight,
+    query_bias,
+    value_bias,
+    mixer_weight,
+    mixer_bias,
+    midnorm_gain,
+    midnorm_shift,
+    expand_weight,
+    expand_bias,
+    shrink_weight,
+    shrink_bias,
+):
+    nf, nc, each = net.nf, net.nc, net.each
+    low, wide = jnp.bfloat16, jnp.float32
+    _, stretch_len, width = inputs.shape
+    heads_each = -(-(width // HEAD) // nf)
+    span = heads_each * HEAD
+    slots = slot_width(heads_each)
+    rows_all = nc * stretch_len
+    rows_own = each * stretch_len
+    shard = lax.axis_index("fsdp")
+    place = lax.axis_index("ctx")
+    in_order = net.blocks_in_order()
+    inverse = jnp.sum(
+        jnp.where(
+            jnp.stack([stretch_order[k] for k in in_order])[None, :] == jnp.arange(nc, dtype=jnp.int32)[:, None],
+            jnp.arange(nc, dtype=jnp.int32)[None, :],
+            0,
+        ),
+        axis=1,
+    ).astype(jnp.int32)
+
+    narrow = prenorm_gain.shape[0]
+    unit_each = expand_bias.shape[0] // nf
+
+    own_tokens = net.swap_blocks(inputs, net.to_column).reshape(rows_own, width)
+    own_tangent = net.swap_blocks(cotangent, net.to_column).reshape(rows_own, width)
+
+    depth = joint_weight.shape[0]
+    thin = -(-depth // (8 * nc)) * 8
+    out_each = shrink_weight.shape[1]
+    seg_own = jnp.pad(segments.astype(low), ((0, 16 - each), (0, 0)))
+    joint_tall = jnp.pad(joint_weight, ((0, nc * thin - depth), (0, 0)))
+    joint_pieces, expand_pieces, shrink_pieces, seg_pieces = net.trade(
+        [
+            joint_tall.reshape(nc, thin, joint_weight.shape[1]),
+            expand_weight.T.reshape(nf, unit_each, depth),
+            shrink_weight.reshape(each, nf, unit_each, out_each)
+            .transpose(1, 0, 2, 3)
+            .reshape(nf, each * unit_each, out_each),
+            jnp.broadcast_to(seg_own[None], (nf,) + seg_own.shape),
+        ],
+        ["ctx", "fsdp", "fsdp", "fsdp"],
+    )
+    small_parts = (
+        prenorm_gain, prenorm_shift, query_bias, value_bias, mixer_bias,
+        midnorm_gain, midnorm_shift, shrink_bias, expand_bias,
+    )
+    small_own = jnp.concatenate(small_parts)
+    small_count = small_own.shape[0]
+    small_rows = -(-small_count // (16 * LANES)) * 16
+    small_own = jnp.pad(small_own, (0, small_rows * LANES - small_count))
+    small_own = jnp.concatenate(
+        [small_own.reshape(small_rows, LANES), seg_pieces[:, :each].reshape(nf * each, LANES)]
+    )
+    small_own = jnp.pad(small_own, ((0, -small_own.shape[0] % 16), (0, 0)))
+    joint_pieces = joint_pieces.transpose(1, 0, 2).reshape(thin, 3, width)
+    joint_pieces = net.trade_fsdp(joint_split(joint_pieces, nf, heads_each))
+    expand_pieces = expand_pieces.transpose(1, 0, 2).reshape(unit_each, width)
+    shrink_pieces = shrink_pieces.reshape(nc * unit_each, out_each).T
+
+    step = span - mixer_weight.shape[0]
+    most = step * (nf - 1)
+    above = lax.ppermute(
+        mixer_weight[:most], "fsdp", [(f, (f - 1) % nf) for f in range(nf)]
+    )
+    tall = jnp.concatenate([mixer_weight, above, jnp.zeros_like(above)])
+    mixer_rows = lax.dynamic_slice_in_dim(tall, step * shard, span, 0)
+    kept = shard * span + jnp.arange(span, dtype=jnp.int32) < width
+    mixer_rows = jnp.where(kept[:, None], mixer_rows, jnp.zeros_like(mixer_rows))
+    mixer_pieces = jnp.pad(mixer_rows.T, ((0, 0), (0, slots - span)))
+
+    joint, mixer, expand, shrink, small_all, tokens, tangent = net.startup(
+        [
+            joint_pieces.reshape(nf * thin, 3 * slots),
+            mixer_pieces,
+            expand_pieces,
+            shrink_pieces,
+            small_own,
+        ],
+        [own_tokens, own_tangent],
+    )
+    expand = expand.reshape(nc * unit_each, width)
+    joint = joint.reshape(nc, nf, thin, 3 * slots).transpose(1, 0, 2, 3)
+    joint = joint.reshape(nf, nc * thin, 3 * slots)[:, :depth].reshape(width, 3 * slots)
+    mixer = mixer.reshape(width, slots)
+    shrink = shrink.reshape(width, nc * unit_each)
+    tokens = tokens.reshape(rows_all, width)
+    tangent = tangent.reshape(rows_all, width)
+    seg_blocks = lax.dynamic_index_in_dim(
+        small_all[:, small_rows : small_rows + nf * each],
+        net.sequence_of(place),
+        1,
+        keepdims=False,
+    ).astype(jnp.int32)
+    seg_blocks = jnp.stack([seg_blocks[k] for k in in_order])
+    small_all = small_all[:, :small_rows].reshape(nc, small_rows * LANES)[:, :small_count]
+    smalls = [
+        small_all[:, k * narrow : (k + 1) * narrow].reshape(width).astype(wide) for k in range(8)
+    ]
+    gain_one, shift_one, qbias, vbias, mbias, gain_two, shift_two, sbias = smalls
+    ebias = lax.dynamic_index_in_dim(
+        small_all[:, 8 * narrow :].reshape(nc, nf, unit_each), shard, 1, keepdims=False
+    ).reshape(nc * unit_each).astype(wide)
+    joint_bias = lax.dynamic_index_in_dim(
+        joint_split(
+            jnp.stack([qbias, jnp.zeros_like(qbias), vbias])[None], nf, heads_each
+        ),
+        shard, 0, keepdims=False,
+    )
+
+    token_values = tokens.astype(wide)
+    unit_one, _ = normalize(token_values)
+    normed = (unit_one * gain_one + shift_one).astype(low)
+    qkv = (
+        jnp.dot(normed, joint, preferred_element_type=wide) + joint_bias
+    ).astype(low)
+    attended, turned, lse = attend_forward(inverse, seg_blocks, qkv)
+    branch = net.scatter_fsdp(times_transposed(attended, mixer).astype(low))
+    middle = own_tokens.astype(wide) + branch + mbias
+    unit_two, inverse_two = normalize(middle)
+    second_own = (unit_two * gain_two + shift_two).astype(low)
+    second = net.gather_fsdp(second_own)
+    expanded = times_transposed(second, expand) + ebias
+    active, slope = gelu_parts(expanded)
+    active = active.astype(low)
+    lifted = net.scatter_fsdp(times_transposed(active, shrink).astype(low))
+    out_rows = (middle + lifted + sbias).astype(low)
+    block_output = net.swap_blocks(out_rows.reshape(each, stretch_len, width), net.to_origin)
+
+    shrink_grad = net.scatter_ctx(
+        outer_sum(tangent, active).astype(low).reshape(nc, out_each, nc * unit_each)
+    )
+    active_grad = jnp.dot(tangent, shrink, preferred_element_type=wide)
+    expand_delta = (active_grad * slope).astype(low)
+    expand_grad = net.scatter_ctx(
+        outer_sum(expand_delta, second).astype(low).reshape(nc, unit_each, width)
+    )
+    second_grad = net.scatter_fsdp(
+        jnp.dot(expand_delta, expand, preferred_element_type=wide).astype(low)
+    )
+    middle_delta = own_tangent.astype(wide) + normalize_back(
+        second_grad, gain_two, unit_two, inverse_two
+    )
+    branch_own = middle_delta.astype(low)
+    branch_delta = net.gather_fsdp(branch_own)
+    attended_delta = jnp.dot(branch_delta, mixer, preferred_element_type=wide).astype(low)
+    mixer_rows = outer_sum(branch_delta, attended).astype(low).reshape(nc, out_each, slots)
+    joint_delta = attend_backward(inverse, seg_blocks, qkv, attended_delta, turned, lse)
+    normed_grad = net.scatter_fsdp(times_transposed(joint_delta, joint).astype(low))
+    unit_own, inverse_own = normalize(own_tokens.astype(wide))
+    input_rows = middle_delta + normalize_back(normed_grad, gain_one, unit_own, inverse_own)
+    input_gradient = net.swap_blocks(
+        input_rows.astype(low).reshape(each, stretch_len, width), net.to_origin
+    ).astype(wide)
+
+    mine = jnp.arange(nf, dtype=jnp.int32) == shard
+    sums = jnp.sum(joint_delta.astype(wide), axis=0).reshape(3, slots)[:, :span]
+    spread = jnp.where(mine[None, :, None], sums[:, None, :], 0.0).reshape(3, nf * span)
+    unit_sums = jnp.sum(expand_delta.astype(wide), axis=0).reshape(nc, 1, unit_each)
+    unit_sums = jnp.where(mine[None, :, None], unit_sums, 0.0).reshape(nc, nf * unit_each)
+    vectors = (
+        jnp.sum(normed_grad * unit_own, axis=0),
+        jnp.sum(normed_grad, axis=0),
+        spread[0, :width],
+        spread[2, :width],
+        jnp.sum(branch_own.astype(wide), axis=0),
+        jnp.sum(second_grad * unit_two, axis=0),
+        jnp.sum(second_grad, axis=0),
+        jnp.sum(own_tangent.astype(wide), axis=0),
+    )
+    stacked = jnp.concatenate([v.reshape(nc, narrow) for v in vectors] + [unit_sums], axis=1)
+    stacked = jnp.pad(stacked, ((0, 0), (0, small_rows * LANES - small_count)))
+    small_blocks = stacked.astype(low).reshape(nc, small_rows, LANES)
+
+    joint_rows = outer_sum(normed, joint_delta).astype(low)
+    joint_rows = jnp.pad(
+        joint_rows.reshape(nf, depth, 3 * slots), ((0, 0), (0, nc * thin - depth), (0, 0))
+    )
+    joint_rows = joint_rows.reshape(nf, nc, thin, 3 * slots).transpose(1, 0, 2, 3)
+    joint_grad, mixer_grad, small_grad = net.ring_scatter(
+        [joint_rows.reshape(nc, nf * thin, 3 * slots), mixer_rows, small_blocks]
+    )
+    joint_pieces, expand_pieces, shrink_pieces, small_pieces = net.trade(
+        [
+            joint_grad.reshape(nf, thin, 3 * slots),
+            expand_grad.reshape(unit_each, nf, depth).transpose(1, 0, 2),
+            shrink_grad.T.reshape(nf, each * unit_each, out_each),
+            jnp.broadcast_to(small_grad[None], (nf,) + small_grad.shape),
+        ],
+        ["fsdp"] * 4,
+    )
+    joint_pieces = joint_join(joint_pieces, heads_each, width)
+    joint_pieces = joint_pieces.reshape(thin, nc, joint_weight.shape[1]).transpose(1, 0, 2)
+    joint_gradient = (
+        net.trade_ctx(joint_pieces)
+        .reshape(nc * thin, joint_weight.shape[1])[:depth]
+        .astype(wide)
+    )
+    expand_gradient = expand_pieces.reshape(nf * unit_each, depth).T.astype(wide)
+    shrink_pieces = shrink_pieces.reshape(nf, each, unit_each, out_each).transpose(1, 0, 2, 3)
+    shrink_gradient = shrink_pieces.reshape(shrink_weight.shape).astype(wide)
+
+    own_rows = mixer_grad[:, :span].T
+    below = lax.dynamic_slice_in_dim(
+        jnp.pad(own_rows, ((0, most), (0, 0))), mixer_weight.shape[0] - step * shard, most, 0
+    )
+    below = lax.ppermute(below, "fsdp", [(f, (f + 1) % nf) for f in range(nf)])
+    moved = lax.dynamic_slice_in_dim(
+        jnp.pad(own_rows, ((most, 0), (0, 0))), most - step * shard, mixer_weight.shape[0], 0
+    )
+    first_rows = jnp.arange(mixer_weight.shape[0], dtype=jnp.int32)[:, None] < step * shard
+    below = jnp.pad(below, ((0, mixer_weight.shape[0] - most), (0, 0)))
+    mixer_gradient = jnp.where(first_rows, below, moved).astype(wide)
+
+    small_sum = jnp.sum(small_pieces.astype(wide), axis=0).reshape(small_rows * LANES)
+    outs = [small_sum[k * narrow : (k + 1) * narrow] for k in range(8)]
+    return (
+        block_output,
+        input_gradient,
+        outs[0],
+        outs[1],
+        joint_gradient,
+        outs[2],
+        outs[3],
+        mixer_gradient,
+        outs[4],
+        outs[5],
+        outs[6],
+        expand_gradient,
+        small_sum[8 * narrow : small_count],
+        shrink_gradient,
+        outs[7],
+    )
+
+
 def solution(mesh):
     in_specs = (
         P("fsdp", "ctx", None),
@@ -621,4 +1714,16 @@
         P("fsdp", "ctx"),
         P("ctx"),
     )
-    return jax.shard_map(local, mesh=mesh, in_specs=in_specs, out_specs=out_specs, check_vma=False)
+
+    def run(*arrays):
+        nf, nc = mesh.shape["fsdp"], mesh.shape["ctx"]
+        whole_each = arrays[0].shape[0] == nc and (nf, nc) == (4, 8)
+        if whole_each and arrays[0].shape[1] == nc * STRETCH:
+            body = functools.partial(local_fast, Net(nf, nc))
+        else:
+            body = local
+        return jax.shard_map(
+            body, mesh=mesh, in_specs=in_specs, out_specs=out_specs, check_vma=False
+        )(*arrays)
+
+    return run

time: 2580 us -> 928 us (0.36)
  waiting for transfers between devices: 1820 us -> 19.4 us
  Pallas kernels: 0 us -> 607 us
  blocking collectives: 232 us -> 0 us
  matrix products: 334 us -> 104 us
    all_gather x16 -> x0, waiting for transfers between devices: 752 us -> none  [the longest x2 129 us: local(): lax.all_gather(forward_values_local, 'ctx', axis=1, tiled=True)]
    unnamed x31 -> x3, waiting for transfers between devices: 718 us -> 0.03 us
    pallas_call x0 -> x14, Pallas kernels: none -> 607 us  [the longest x12 538 us: call(): pl.pallas_call(kernel, out_shape=outs, in_specs=in_specs, out_specs=out_s...]
    reduce_scatter x1, waiting for transfers between devices: 346 us -> 0.01 us  [scatter_ctx(): return lax.psum_scatter(blocks, 'ctx', scatter_dimension=0)]
    dot_general x36 -> x4, matrix products: 220 us -> 38.7 us  [the longest x1 15.8 us: local_fast(): active_grad = jnp.dot(tangent, shrink, preferred_element_type=wide)]
    all_gather x5 -> x0, blocking collectives: 151 us -> none  [the longest x2 66.8 us: backward_micro(): lax.all_gather(log_rows, 'ctx', axis=1, tiled=True)]
    unnamed x2 -> x0, blocking collectives: 74.6 us -> none
    unnamed x211 -> x76, local copies, waits for them, and re-layouts: 55.1 us -> 9.36 us
  transfers between devices with their start and end apart: 24 -> 12, of which waited for: 17 -> 1; matrix products, arithmetic and copies ran while one was open for 19% -> 17% of each run, Pallas kernels for 0% -> 31%
where the time goes in v1:
time: 928 us; the launch traced here: 916 us
  Pallas kernels  607 us (65%)
  local copies, waits for them, and re-layouts  110 us (12%)
  matrix products  104 us (11%)
  other arithmetic  40.1 us (4%)
  starting transfers between devices  20.3 us (2%)
  waiting for transfers between devices  19.4 us (2%)
  between operations  15.6 us (2%)
    pallas_call x12, Pallas kernels, call(): pl.pallas_call(kernel, out_shape=outs, in_specs=in_specs, out_specs=out_s...  538 us
    dot_general x4, matrix products, times_transposed(): lax.dot_general(left, right, (((1,), (1,)), ((), ())), preferred_element_...  36 us
    pallas_call x1, Pallas kernels, attend_forward(): pl.pallas_call(attend_forward_kernel, grid_spec=pltpu.PrefetchScalarGridS...  34.5 us
    pallas_call x1, Pallas kernels, attend_backward(): pl.pallas_call(attend_backward_kernel, grid_spec=pltpu.PrefetchScalarGrid...  34.2 us
    dot_general x4, matrix products, outer_sum(): lax.dot_general(left, right, (((0,), (0,)), ((), ())), preferred_element_...  29.5 us
    ppermute x8, waiting for transfers between devices, swap_blocks(): got.append(lax.ppermute(piece, ('fsdp', 'ctx'), pairs))  19.4 us
  transfers between devices with their start and end apart: 12, of which 1 were waited for; matrix products, arithmetic and copies ran while one was open for 17% of the time, Pallas kernels for 31%

profile of v1, /device:TPU:0, one launch (start us, length us, event | category | flops | bytes accessed | tf_op | source)
XLA Modules:
  0.0 916.3 jit_solution(9332124032679729468)
XLA Ops:
  9.2 2.4 collective-permute-start.2
  13.6 4.9 collective-permute-start
  18.5 2.1 dynamic-slice_bitcast_fusion.1
  20.7 4.9 collective-permute-start.3
  33.0 33.7 %trade.4 = (bf16[8,56,640]{2,1,0:T(8,128)(2,1)}, bf16[4,200,512]{2,1,0:T(8,128)(2,1)}, bf16[4,400,256]{2,1,0:T(8,128)(2,1)}, bf16[4,16,128]{2,1,0:T(8,128)(2,1)}) custom-call(bf16[8,56,640]{2,1,0:T(8,128)(2,1)} %pad.79.refs_0_, bf16[4,200,512]{2,1,0:T(8,128)(2,1)} %pad.80.refs_1_, bf16[4,400,256]{2,1,0:T(8,128)(2,1)} %pad.81.refs_2_, ...), custom_call_target="tpu_custom_call" | custom-call | tf_op jit(solution)/shard_map/trade/pallas_call | solution.py:1305
  73.6 10.2 %trade.5 = bf16[4,56,1536]{2,1,0:T(8,128)(2,1)} custom-call(bf16[4,56,1536]{2,1,0:T(8,128)(2,1)} %reshape.451.refs_0_), custom_call_target="tpu_custom_call" | custom-call | tf_op jit(solution)/shard_map/trade/pallas_call | solution.py:1305
  97.9 177.4 %startup.1 = (bf16[8,224,1536]{2,1,0:T(8,128)(2,1)}, bf16[8,200,512]{2,1,0:T(8,128)(2,1)}, bf16[8,200,1600]{2,1,0:T(8,128)(2,1)}, bf16[8,200,1600]{2,1,0:T(8,128...) custom-call(bf16[224,1536]{1,0:T(8,128)(2,1)} %bitcast.203, ...), custom_call_target="tpu_custom_call" | custom-call | tf_op jit(solution)/shard_map/startup/pallas_call | solution.py:1305
  277.3 3.0 copy.123
  280.3 2.8 slice.232
  290.9 7.3 add_convert_fusion.1.qkv_ref
  298.2 34.5 %attend_forward.1 = (bf16[1024,512]{1,0:T(8,128)(2,1)}, f32[4,128,1024]{2,1,0:T(8,128)}, f32[4,2,1024]{2,1,0:T(2,128)}) custom-call(s32[8]{0:T(128)} %select_reduce_fusion.inv_ref, s32[8,128]{1,0:T(8,128)} %copy-done.15, s32[1024,1]{1,0:T(8,128)} %copy.124.seg_col_ref, bf16[1024,1536]{1,0:T(8,128)(2,1)} %add_convert_fusion.1.qkv_ref), custom_call_target="tpu_custom_call" | custom-call | tf_op jit(solution)/shard_map/attend_forward/pallas_call | solution.py:814
  332.8 5.4 convolution_convert_fusion.6
  338.1 5.4 copy.125
  343.6 26.3 %scatter_fsdp.4 = f32[256,1600]{1,0:T(8,128)} custom-call(bf16[4,256,1600]{2,1,0:T(8,128)(2,1)} %bitcast.182), custom_call_target="tpu_custom_call" | custom-call | tf_op jit(solution)/shard_map/scatter_fsdp/pallas_call | solution.py:1305
  374.4 24.1 %gather_fsdp.2 = bf16[4,256,1600]{2,1,0:T(8,128)(2,1)} custom-call(bf16[256,1600]{1,0:T(8,128)(2,1)} %add_convert_fusion.3.own_ref), custom_call_target="tpu_custom_call" | custom-call | tf_op jit(solution)/shard_map/gather_fsdp/pallas_call | solution.py:1305
  398.5 9.5 %fusion.45 = f32[1024,1600]{0,1:T(8,128)S(1)} fusion(bf16[1024,1600]{1,0:T(8,128)(2,1)} %bitcast.194, bf16[1600,1600]{1,0:T(8,128)(2,1)} %bitcast.234), kind=kOutput, calls=%fused_computation.168 | convolution fusion | flops 5242880000 | bytes 14950400 | tf_op jit(solution)/shard_map/dot_general | solution.py:45
  408.0 10.4 %convolution_convert_fusion = bf16[1600,1600]{1,0:T(8,128)(2,1)} fusion(bf16[1024,1600]{1,0:T(8,128)(2,1)S(1)} %bitcast.237, f32[1024,1600]{0,1:T(8,128)S(1)} %fusion.45, f32[1600]{0:T(1024)S(1)} %reshape.505), kind=kOutput, calls=%fused_computation.6 | convolution fusion | flops 5261824000 | bytes 14956800 | tf_op jit(solution)/shard_map/dot_general | solution.py:51
  418.4 8.3 copy.136
  427.3 15.8 %convert_reduce_fusion = (bf16[1600]{0:T(1024)(128)(2,1)S(1)}, bf16[1024,1600]{0,1:T(8,128)(2,1)S(1)}) fusion(f32[1024,1600]{0,1:T(8,128)} %copy-done.32, f32[1600]{0:T(1024)S(1)} %reshape.505, bf16[1024,1600]{1,0:T(8,128)(2,1)} %bitcast.236, bf16[1600,1600]{1,0:T(8,128)(2,1)} %bitcast.232), kind=kOutput, calls=%fused_computation.23 | convolution fusion | flops 5278923264 | bytes 18236800 | tf_op jit(solution)/shard_map/dot_general | solution.py:1577
  444.8 10.1 %convolution_convert_fusion.5 = bf16[1024,1600]{0,1:T(8,128)(2,1)} fusion(bf16[1024,1600]{0,1:T(8,128)(2,1)S(1)} %get-tuple-element.179, bf16[1600,1600]{1,0:T(8,128)(2,1)} %bitcast.235), kind=kOutput, calls=%fused_computation.30 | convolution fusion | flops 5244518400 | bytes 11673600 | tf_op jit(solution)/shard_map/dot_general | solution.py:1583
  455.0 5.5 copy.129
  460.4 26.3 %scatter_fsdp.6 = f32[256,1600]{1,0:T(8,128)} custom-call(bf16[4,256,1600]{2,1,0:T(8,128)(2,1)} %bitcast.183), custom_call_target="tpu_custom_call" | custom-call | tf_op jit(solution)/shard_map/scatter_fsdp/pallas_call | solution.py:1305
  486.8 11.8 %convolution_convert_fusion.3 = bf16[1024,1600]{0,1:T(8,128)(2,1)} fusion(bf16[1600,1600]{1,0:T(8,128)(2,1)} %bitcast.233, f32[1024,1600]{0,1:T(8,128)} %copy-done.32, f32[1600]{0:T(1024)S(1)} %reshape.505), kind=kOutput, calls=%fused_computation.28 | convolution fusion | flops 5260902400 | bytes 14956800 | tf_op jit(solution)/shard_map/dot_general | solution.py:45
  498.6 5.5 copy.126
  504.1 26.1 %scatter_fsdp.5 = f32[256,1600]{1,0:T(8,128)} custom-call(bf16[4,256,1600]{2,1,0:T(8,128)(2,1)} %bitcast.184), custom_call_target="tpu_custom_call" | custom-call | tf_op jit(solution)/shard_map/scatter_fsdp/pallas_call | solution.py:1305
  530.2 10.3 %convolution_convert_fusion.1 = bf16[1600,1600]{1,0:T(8,128)(2,1)} fusion(bf16[1024,1600]{0,1:T(8,128)(2,1)} %copy-done.33, bf16[1024,1600]{1,0:T(8,128)(2,1)} %bitcast.195), kind=kOutput, calls=%fused_computation.7 | convolution fusion | flops 5245440000 | bytes 11673600 | tf_op jit(solution)/shard_map/dot_general | solution.py:51
  540.6 4.1 multiply_reduce_fusion.1
  545.1 4.5 fusion.40
  556.5 4.9 collective-permute-start.5
  561.4 24.1 %gather_fsdp.3 = bf16[4,256,1600]{2,1,0:T(8,128)(2,1)} custom-call(bf16[256,1600]{1,0:T(8,128)(2,1)} %get-tuple-element.131.own_ref), custom_call_target="tpu_custom_call" | custom-call | tf_op jit(solution)/shard_map/gather_fsdp/pallas_call | solution.py:1305
  585.5 5.5 convolution_convert_fusion.8.grad_ref
  591.0 34.2 %attend_backward.1 = bf16[1024,1536]{1,0:T(8,128)(2,1)} custom-call(s32[8]{0:T(128)} %select_reduce_fusion.inv_ref, s32[8,128]{1,0:T(8,128)} %copy-done.15, s32[1024,1]{1,0:T(8,128)} %copy.124.seg_col_ref, bf16[1024,1536]{1,0:T(8,128)(2,1)} %add_convert_fusion.1.qkv_ref, bf16[1024,512]{1,0:T(8,128)(2,1)} %convolution_convert_fusion.8.grad_ref, ...), custom_call_target="tpu_custom_call" | custom-call | tf_op jit(solution)/shard_map/attend_backward/pallas_call | solution.py:849
  625.2 2.4 convert_reduce_fusion.2
  628.0 9.3 %convolution_convert_fusion.4 = bf16[1024,1600]{0,1:T(8,128)(2,1)} fusion(bf16[1024,1536]{1,0:T(8,128)(2,1)} %attend_backward.1, bf16[1600,1536]{1,0:T(8,128)(2,1)} %bitcast.190), kind=kOutput, calls=%fused_computation.29 | convolution fusion | flops 5034803200 | bytes 11337728 | tf_op jit(solution)/shard_map/dot_general | solution.py:45
  637.3 5.5 copy.131
  642.8 26.5 %scatter_fsdp.7 = f32[256,1600]{1,0:T(8,128)} custom-call(bf16[4,256,1600]{2,1,0:T(8,128)(2,1)} %bitcast.185), custom_call_target="tpu_custom_call" | custom-call | tf_op jit(solution)/shard_map/scatter_fsdp/pallas_call | solution.py:1305
  670.7 2.5 fusion.21
  676.0 5.7 convolution_convert_fusion.2
  682.2 3.3 copy.134
  686.4 3.1 convolution_convert_fusion.7
  689.5 104.8 %ring_scatter.1 = (bf16[224,1536]{1,0:T(8,128)(2,1)}, bf16[200,512]{1,0:T(8,128)(2,1)}, bf16[32,128]{1,0:T(8,128)(2,1)}) custom-call(bf16[8,224,1536]{2,1,0:T(8,128)(2,1)} %bitcast.178, bf16[8,200,512]{2,1,0:T(8,128)(2,1)} %bitcast.208, bf16[8,32,128]{2,1,0:T(8,128)(2,1)} %bitcast.221), custom_call_target="tpu_custom_call" | custom-call | tf_op jit(solution)/shard_map/ring_scatter/pallas_call | solution.py:1305
  805.2 19.4 %collective-permute-done.8 = bf16[128,1600]{0,1:T(8,128)(2,1)S(1)} collective-permute-done((bf16[128,1600]{0,1:T(8,128)(2,1)}, bf16[128,1600]{0,1:T(8,128)(2,1)S(1)}, u32[]{:S(2)}, u32[]{:S(2)}) %collective-permute-start.8) | collective-permute-done | bytes 409632 | tf_op jit(solution)/shard_map/ppermute | solution.py:1341
  827.1 2.2 pad.93.refs_2_
  829.3 3.2 reshape_reduce_scatter.3
  834.2 43.4 %trade.6 = (bf16[4,56,1536]{2,1,0:T(8,128)(2,1)}, bf16[4,200,512]{2,1,0:T(8,128)(2,1)}, bf16[4,400,256]{2,1,0:T(8,128)(2,1)}, bf16[4,32,128]{2,1,0:T(8,128)(2,1)}) custom-call(bf16[4,56,1536]{2,1,0:T(8,128)(2,1)} %bitcast.215, bf16[4,200,512]{2,1,0:T(8,128)(2,1)} %pad.92.refs_1_, bf16[4,400,256]{2,1,0:T(8,128)(2,1)} %pad.93.refs_2_, ...), custom_call_target="tpu_custom_call" | custom-call | tf_op jit(solution)/shard_map/trade/pallas_call | solution.py:1305
  879.7 2.5 reshape.495
  886.3 14.8 %trade.7 = bf16[8,56,640]{2,1,0:T(8,128)(2,1)} custom-call(bf16[8,56,640]{2,1,0:T(8,128)(2,1)} %pad.94.refs_0_), custom_call_target="tpu_custom_call" | custom-call | tf_op jit(solution)/shard_map/trade/pallas_call | solution.py:1305
  906.2 2.8 reshape.508
  (249 shorter events, 87.8 us)
Async XLA Ops:
  7.2 19.0 %copy-start.31 = (s32[2,128]{1,0:T(2,128)S(1)}, s32[2,128]{1,0:T(2,128)}, u32[]{:S(2)}) copy-start(s32[2,128]{1,0:T(2,128)} %param.21) | copy-start | bytes 3076
  7.2 19.0 %copy-start.17 = (s32[8]{0:T(128)S(1)}, s32[8]{0:T(128)}, u32[]{:S(2)}) copy-start(s32[8]{0:T(128)} %param.22) | copy-start | bytes 100
  7.2 19.7 %copy-start.28 = (bf16[200]{0:T(256)(128)(2,1)S(1)}, bf16[200]{0:T(256)(128)(2,1)}, u32[]{:S(2)}) copy-start(bf16[200]{0:T(256)(128)(2,1)} %param.35) | copy-start | bytes 1204
  7.2 19.7 %copy-start.20 = (bf16[800]{0:T(1024)(128)(2,1)S(1)}, bf16[800]{0:T(1024)(128)(2,1)}, u32[]{:S(2)}) copy-start(bf16[800]{0:T(1024)(128)(2,1)} %param.33) | copy-start | bytes 4804
  7.2 19.7 %copy-start.27 = (bf16[200]{0:T(256)(128)(2,1)S(1)}, bf16[200]{0:T(256)(128)(2,1)}, u32[]{:S(2)}) copy-start(bf16[200]{0:T(256)(128)(2,1)} %param.31) | copy-start | bytes 1204
  7.2 19.7 %copy-start.26 = (bf16[200]{0:T(256)(128)(2,1)S(1)}, bf16[200]{0:T(256)(128)(2,1)}, u32[]{:S(2)}) copy-start(bf16[200]{0:T(256)(128)(2,1)} %param.30) | copy-start | bytes 1204
  7.2 19.7 %copy-start.25 = (bf16[200]{0:T(256)(128)(2,1)S(1)}, bf16[200]{0:T(256)(128)(2,1)}, u32[]{:S(2)}) copy-start(bf16[200]{0:T(256)(128)(2,1)} %param.29) | copy-start | bytes 1204
  7.3 19.7 %copy-start.24 = (bf16[200]{0:T(256)(128)(2,1)S(1)}, bf16[200]{0:T(256)(128)(2,1)}, u32[]{:S(2)}) copy-start(bf16[200]{0:T(256)(128)(2,1)} %param.27) | copy-start | bytes 1204
  7.3 19.7 %copy-start.23 = (bf16[200]{0:T(256)(128)(2,1)S(1)}, bf16[200]{0:T(256)(128)(2,1)}, u32[]{:S(2)}) copy-start(bf16[200]{0:T(256)(128)(2,1)} %param.26) | copy-start | bytes 1204
  7.3 19.7 %copy-start.22 = (bf16[200]{0:T(256)(128)(2,1)S(1)}, bf16[200]{0:T(256)(128)(2,1)}, u32[]{:S(2)}) copy-start(bf16[200]{0:T(256)(128)(2,1)} %param.24) | copy-start | bytes 1204
  7.3 19.7 %copy-start.21 = (bf16[200]{0:T(256)(128)(2,1)S(1)}, bf16[200]{0:T(256)(128)(2,1)}, u32[]{:S(2)}) copy-start(bf16[200]{0:T(256)(128)(2,1)} %param.23) | copy-start | bytes 1204
  7.3 19.9 %copy-start.14 = (bf16[400,600]{1,0:T(8,128)(2,1)S(1)}, bf16[400,600]{1,0:T(8,128)(2,1)}, u32[]{:S(2)}) copy-start(bf16[400,600]{1,0:T(8,128)(2,1)} %param.25) | copy-start | bytes 1440004
  7.3 20.8 %copy-start.12 = (bf16[400,800]{1,0:T(8,128)(2,1)S(1)}, bf16[400,800]{1,0:T(8,128)(2,1)}, u32[]{:S(2)}) copy-start(bf16[400,800]{1,0:T(8,128)(2,1)} %param.32) | copy-start | bytes 1920004
  7.3 819.8 %reduce-scatter.5.cloned.1.call-start = ((), (), s32[]{:S(2)}) async-start(), calls=%async_computation.2 | async-start | bytes 7372800 | tf_op jit(solution)/shard_map/reduce_scatter | solution.py:1385
  9.2 79.1 %collective-permute-start.2 = (bf16[144,200]{0,1:T(8,128)(2,1)}, bf16[144,200]{0,1:T(8,128)(2,1)}, u32[]{:S(2)}, u32[]{:S(2)}) collective-permute-start(bf16[144,200]{0,1:T(8,128)(2,1)} %slice.228), channel_id=1, source_target_pairs={{0,24},{8,0},{16,8},{24,16},{1,25},{9,1},{17,9},{25,17},{2,26},{10... | collective-permute-start | bytes 172808 | tf_op jit(solution)/shard_map/ppermute | solution.py:1507
  13.6 76.5 %collective-permute-start = (bf16[128,1600]{0,1:T(8,128)(2,1)}, bf16[128,1600]{0,1:T(8,128)(2,1)}, u32[]{:S(2)}, u32[]{:S(2)}) collective-permute-start(bf16[128,1600]{0,1:T(8,128)(2,1)} %get-tuple-element.144), channel_id=1, source_target_pairs={{0,0},{1,2},{2,16},{3,18},{4,8},{5,10},{6,24},{7,26},{8,4},{9,6},{... | collective-permute-start | bytes 1228808 | tf_op jit(solution)/shard_map/ppermute | solution.py:1341
  18.5 10.8 %copy-start.13 = (bf16[1600,200]{0,1:T(8,128)(2,1)S(1)}, bf16[1600,200]{0,1:T(8,128)(2,1)}, u32[]{:S(2)}) copy-start(bf16[1600,200]{0,1:T(8,128)(2,1)} %param.34) | copy-start | bytes 1920004
  18.5 71.6 %collective-permute-start.1 = (bf16[128,1600]{0,1:T(8,128)(2,1)}, bf16[128,1600]{0,1:T(8,128)(2,1)}, u32[]{:S(2)}, u32[]{:S(2)}) collective-permute-start(bf16[128,1600]{0,1:T(8,128)(2,1)} %get-tuple-element.145), channel_id=1, source_target_pairs={{0,2},{1,0},{2,18},{3,16},{4,10},{5,8},{6,26},{7,24},{8,6},{9,4},{... | collective-permute-start | bytes 1228808 | tf_op jit(solution)/shard_map/ppermute | solution.py:1341
  20.7 73.5 %collective-permute-start.3 = (bf16[128,1600]{0,1:T(8,128)(2,1)}, bf16[128,1600]{0,1:T(8,128)(2,1)}, u32[]{:S(2)}, u32[]{:S(2)}) collective-permute-start(bf16[128,1600]{0,1:T(8,128)(2,1)} %get-tuple-element.142), channel_id=1, source_target_pairs={{0,0},{1,2},{2,16},{3,18},{4,8},{5,10},{6,24},{7,26},{8,4},{9,6},{... | collective-permute-start | bytes 1228808 | tf_op jit(solution)/shard_map/ppermute | solution.py:1341
  25.6 68.6 %collective-permute-start.4 = (bf16[128,1600]{0,1:T(8,128)(2,1)}, bf16[128,1600]{0,1:T(8,128)(2,1)}, u32[]{:S(2)}, u32[]{:S(2)}) collective-permute-start(bf16[128,1600]{0,1:T(8,128)(2,1)} %get-tuple-element.143), channel_id=1, source_target_pairs={{0,2},{1,0},{2,18},{3,16},{4,10},{5,8},{6,26},{7,24},{8,6},{9,4},{... | collective-permute-start | bytes 1228808 | tf_op jit(solution)/shard_map/ppermute | solution.py:1341
  70.1 13.7 %copy-start.11 = (bf16[4,400,256]{2,1,0:T(8,128)(2,1)S(1)}, bf16[4,400,256]{2,1,0:T(8,128)(2,1)}, u32[]{:S(2)}) copy-start(bf16[4,400,256]{2,1,0:T(8,128)(2,1)} %get-tuple-element.39) | copy-start | bytes 2457604
  71.0 13.9 %copy-start.10 = (bf16[4,200,512]{2,1,0:T(8,128)(2,1)S(1)}, bf16[4,200,512]{2,1,0:T(8,128)(2,1)}, u32[]{:S(2)}) copy-start(bf16[4,200,512]{2,1,0:T(8,128)(2,1)} %get-tuple-element.38) | copy-start | bytes 2457604
  92.9 5.0 copy-start.5
  280.3 3.7 copy-start
  287.5 2.5 copy-start.15
  288.5 2.4 copy-start.6
  371.9 1.2 copy-start.1
  398.5 9.5 %copy-start.29 = (bf16[4,256,1600]{2,1,0:T(8,128)(2,1)S(1)}, bf16[4,256,1600]{2,1,0:T(8,128)(2,1)}, u32[]{:S(2)}) copy-start(bf16[4,256,1600]{2,1,0:T(8,128)(2,1)} %get-tuple-element.48) | copy-start | bytes 9830404
  408.0 10.4 %copy-start.32 = (f32[1024,1600]{0,1:T(8,128)}, f32[1024,1600]{0,1:T(8,128)S(1)}, u32[]{:S(2)}) copy-start(f32[1024,1600]{0,1:T(8,128)S(1)} %fusion.45) | copy-start | bytes 19660804
  426.7 402.6 %reduce-scatter.7.cloned.1.call-start = ((), (), s32[]{:S(2)}) async-start(), calls=%async_computation.3 | async-start | bytes 5990400
  443.1 1.8 copy-start.33
  555.9 247.4 %collective-permute-start.6 = (bf16[128,1600]{0,1:T(8,128)(2,1)}, bf16[128,1600]{0,1:T(8,128)(2,1)}, u32[]{:S(2)}, u32[]{:S(2)}) collective-permute-start(bf16[128,1600]{0,1:T(8,128)(2,1)} %bitcast.217), channel_id=1, source_target_pairs={{0,1},{1,17},{2,0},{3,16},{4,9},{5,25},{6,8},{7,24},{8,5},{9,21},{... | collective-permute-start | bytes 1228808 | tf_op jit(solution)/shard_map/ppermute | solution.py:1341
  556.5 246.9 %collective-permute-start.5 = (bf16[128,1600]{0,1:T(8,128)(2,1)}, bf16[128,1600]{0,1:T(8,128)(2,1)}, u32[]{:S(2)}, u32[]{:S(2)}) collective-permute-start(bf16[128,1600]{0,1:T(8,128)(2,1)} %bitcast.216), channel_id=1, source_target_pairs={{0,0},{1,16},{2,1},{3,17},{4,8},{5,24},{6,9},{7,25},{8,4},{9,20},{... | collective-permute-start | bytes 1228808 | tf_op jit(solution)/shard_map/ppermute | solution.py:1341
  642.8 26.5 %copy-start.18 = (f32[2,128]{1,0:T(2,128)S(1)}, f32[2,128]{1,0:T(2,128)}, u32[]{:S(2)}) copy-start(f32[2,128]{1,0:T(2,128)} %get-tuple-element.133) | copy-start | bytes 3076
  674.1 1.9 copy-start.4
  682.2 3.3 copy-start.7
  682.2 4.2 copy-start.30
  689.5 106.0 %copy-start.2 = (bf16[2,128,1600]{2,1,0:T(8,128)(2,1)S(1)}, bf16[2,128,1600]{2,1,0:T(8,128)(2,1)}, u32[]{:S(2)}) copy-start(bf16[2,128,1600]{2,1,0:T(8,128)(2,1)} %copy.111) | copy-start | bytes 2457604
  689.5 106.0 %copy-start.3 = (f32[256,1600]{1,0:T(8,128)S(1)}, f32[256,1600]{1,0:T(8,128)}, u32[]{:S(2)}) copy-start(f32[256,1600]{1,0:T(8,128)} %scatter_fsdp.7) | copy-start | bytes 4915204
  795.4 5.9 collective-permute-start.9
  798.9 25.7 %collective-permute-start.8 = (bf16[128,1600]{0,1:T(8,128)(2,1)}, bf16[128,1600]{0,1:T(8,128)(2,1)S(1)}, u32[]{:S(2)}, u32[]{:S(2)}) collective-permute-start(bf16[128,1600]{0,1:T(8,128)(2,1)} %bitcast.56), channel_id=1, source_target_pairs={{0,1},{1,17},{2,0},{3,16},{4,9},{5,25},{6,8},{7,24},{8,5},{9,21},{... | collective-permute-start | bytes 1228808 | tf_op jit(solution)/shard_map/ppermute | solution.py:1341
  800.6 24.0 %collective-permute-start.7 = (bf16[128,1600]{0,1:T(8,128)(2,1)S(1)}, bf16[128,1600]{0,1:T(8,128)(2,1)S(1)}, u32[]{:S(2)}, u32[]{:S(2)}) collective-permute-start(bf16[128,1600]{0,1:T(8,128)(2,1)S(1)} %bitcast.218), channel_id=1, source_target_pairs={{0,0},{1,16},{2,1},{3,17},{4,8},{5,24},{6,9},{7,25},{8,4},{9,20},{... | collective-permute-start | bytes 1228808 | tf_op jit(solution)/shard_map/ppermute | solution.py:1341
  803.3 22.1 %copy-start.19 = (pred[2]{0:T(512)(128)(4,1)S(1)}, pred[2]{0:T(512)(128)(4,1)}, u32[]{:S(2)}) copy-start(pred[2]{0:T(512)(128)(4,1)} %get-tuple-element.180) | copy-start | bytes 10
  827.1 6.5 copy-start.16
  884.3 18.9 %copy-start.9 = (bf16[4,200,512]{2,1,0:T(8,128)(2,1)S(1)}, bf16[4,200,512]{2,1,0:T(8,128)(2,1)}, u32[]{:S(2)}) copy-start(bf16[4,200,512]{2,1,0:T(8,128)(2,1)} %get-tuple-element.56) | copy-start | bytes 2457604
  901.1 4.0 copy-start.8
Sparse Core Ops, SparseCore 0:
  426.8 121.7 reduce-scatter.4
  552.1 146.3 reduce-scatter.6
